TPU v7x, 64 devices: a 2x2x8 block of a 4x4x8 slice. The times are simulated.
64 devices in a mesh: rep: 4 (over x, y), dp: 16 (over z, core).
Axes of the slice: x: 2, y: 2, z: 8, core: 2. Of those that a mesh axis runs over, the one named last changes fastest.
The devices are a block of a 4x4x8 slice.
Arguments:
- x: bfloat16 [64, 1024, 640], P(('rep', 'dp')), parts along dimension 0
- dy: bfloat16 [64, 1024, 640], P(('rep', 'dp')), parts along dimension 0
- w_gate: bfloat16 [2, 640, 4096], replicated
- w_up: bfloat16 [2, 640, 4096], replicated
- w_down: bfloat16 [2, 4096, 640], replicated
- m_w_gate: float32 [2, 640, 4096], replicated
- m_w_up: float32 [2, 640, 4096], replicated
- m_w_down: float32 [2, 4096, 640], replicated
- v_w_gate: float32 [2, 640, 4096], replicated
- v_w_up: float32 [2, 640, 4096], replicated
- v_w_down: float32 [2, 4096, 640], replicated
Outputs:
- output 1: bfloat16 [8, 640, 4096], P('rep'), parts along dimension 0
- output 2: bfloat16 [8, 640, 4096], P('rep'), parts along dimension 0
- output 3: bfloat16 [8, 4096, 640], P('rep'), parts along dimension 0
- output 4: float32 [8, 640, 4096], P('rep'), parts along dimension 0
- output 5: float32 [8, 640, 4096], P('rep'), parts along dimension 0
- output 6: float32 [8, 4096, 640], P('rep'), parts along dimension 0
- output 7: float32 [8, 640, 4096], P('rep'), parts along dimension 0
- output 8: float32 [8, 640, 4096], P('rep'), parts along dimension 0
- output 9: float32 [8, 4096, 640], P('rep'), parts along dimension 0
There are 4 independent parts. A program takes and returns all parts, laid end to end along the dimension named above; an argument that names none is the same for every part.
All inputs are finite; a program needn't handle non-finite values.
Results may differ from a plain program's by a relative error of at most 0.0226.
Values are sent between devices in bfloat16 or wider.
A program may use at most 768 MiB of HBM per device.

v0:
```python
import functools

import jax
import jax.numpy as jnp
from jax import lax
from jax.experimental import pallas as pl
from jax.experimental.pallas import tpu as pltpu
from jax.sharding import PartitionSpec as P


MESH = pl.DeviceIdType.MESH
BF, F32 = jnp.bfloat16, jnp.float32
LANES = 128
TILE = 512
NS, NP, NR = 5, 5, 5
STEPS, STRIDE, LAG = 9, 6, 3
PARTS, AHEAD = 2, 4


def mm(a, b, ca, cb):
    return lax.dot_general(a, b, (((ca,), (cb,)), ((), ())), preferred_element_type=F32)


class Ring:
    def __init__(self, n):
        me = lax.axis_index("dp")
        self.Z = Z = n // 2
        self.z, self.c = z, c = lax.div(me, 2), lax.rem(me, 2)
        ahead = 2 * c - 1
        self.next = 2 * lax.rem(z + ahead + Z, Z) + c
        self.prev = 2 * lax.rem(z - ahead + Z, Z) + c
        self.mate = 2 * z + 1 - c
        down = lax.rem(Z - z, Z)
        self.p = jnp.where(c == 1, z, down)
        self.mate_p = jnp.where(c == 1, down, z)


def grads_kernel(n, layers, x_hbm, dy_hbm, wg_hbm, wu_hbm, wd_hbm, *refs):
    outs, refs = refs[:layers], refs[layers:]
    a, by, h, da, wg, wu, wd, hid, dgate, dup, full, pbuf, on, back, in_sem, w_sem, d_send, d_recv, on_send, on_recv, back_send, back_recv = refs
    at = Ring(n)
    Z, c, p = at.Z, at.c, at.p
    _, T, D = a.shape
    FF = wg_hbm.shape[2]
    NT = FF // TILE
    J = layers * NT
    F0 = (layers - 1) * NT
    HT = TILE // 2
    DR, FR = D // Z, HT // Z
    GC, DC = HT // LANES, D // LANES
    OFF_U, OFF_D = GC * DR, 2 * GC * DR
    RC = T // 4
    NB = min(256, TILE)
    UP = Z // 2
    DOWN = Z - 1 - UP

    def weights(t):
        l = jnp.where(t < F0, lax.div(t, NT), layers - 1 - lax.div(t - F0, NT))
        f, b = lax.rem(t, NT), lax.rem(t, 2)
        copies = []
        for x in range(2):
            src = pl.ds(pl.multiple_of(x * (FF // 2) + f * HT, HT), HT)
            dst = pl.ds(x * HT, HT)
            copies += [
                pltpu.make_async_copy(wg_hbm.at[l, :, src], wg.at[b, :, dst], w_sem.at[b, x, 0]),
                pltpu.make_async_copy(wu_hbm.at[l, :, src], wu.at[b, :, dst], w_sem.at[b, x, 1]),
                pltpu.make_async_copy(wd_hbm.at[l, src, :], wd.at[b, dst, :], w_sem.at[b, x, 2]),
            ]
        return copies

    def next_weights(t):
        for copy in weights(t):
            copy.wait()

        @pl.when(t + 1 < F0 + J)
        def _():
            for copy in weights(t + 1):
                copy.start()

    def by_rows(size, body):
        size = min(size, T)

        def block(k, _):
            body(pl.ds(pl.multiple_of(k * size, size), size))
            return 0

        lax.fori_loop(0, T // size, block, 0)

    def norm(l):
        def of(rows):
            wide = h[l, rows, :].astype(F32)
            a[l, rows, :] = (wide * lax.rsqrt(jnp.mean(wide * wide, -1, keepdims=True) + 1e-6)).astype(BF)

        by_rows(128, of)

    x_in = pltpu.make_async_copy(x_hbm.at[0], h.at[0], in_sem.at[0])
    dy_in = pltpu.make_async_copy(dy_hbm.at[0], by.at[layers - 1], in_sem.at[1])
    x_in.start()
    for copy in weights(0):
        copy.start()
    dy_in.start()
    bar = pltpu.get_barrier_semaphore()
    for other in (at.next, at.prev, at.mate):
        pl.semaphore_signal(bar, inc=1, device_id={"dp": other}, device_id_type=MESH)
    x_in.wait()
    norm(0)

    def forward(t, _):
        l, f, b = lax.div(t, NT), lax.rem(t, NT), lax.rem(t, 2)
        next_weights(t)

        @pl.when(f == 0)
        def _():
            da[...] = jnp.zeros_like(da)

        for w in range(4):
            rows = pl.ds(w * RC, RC)
            ar = a[l, rows, :]
            for nb in range(0, TILE, NB):
                cols = pl.ds(nb, NB)
                g = mm(ar, wg[b, :, cols], 1, 0)
                u = mm(ar, wu[b, :, cols], 1, 0)
                hid[rows, cols] = (g * (1 / (1 + jnp.exp(-g))) * u).astype(BF)
            da[rows, :] += mm(hid[rows, :], wd[b], 1, 0)

        @pl.when(f == NT - 1)
        def _():
            def of(rows):
                h[l + 1, rows, :] = (h[l, rows, :].astype(F32) + da[rows, :].astype(BF).astype(F32)).astype(BF)

            by_rows(128, of)
            norm(l + 1)

        return 0

    lax.fori_loop(0, F0, forward, 0)
    dy_in.wait()
    pl.semaphore_wait(bar, 3)

    def piece(i, w):
        t = i + F0
        l, f, b, slot = layers - 1 - lax.div(i, NT), lax.rem(i, NT), lax.rem(t, 2), lax.rem(i, NS)
        if w == 0:
            next_weights(t)
        if w < 4:
            rows = pl.ds(w * RC, RC)
            ar, br = a[l, rows, :], by[l, rows, :]
            for nb in range(0, TILE, NB):
                cols = pl.ds(nb, NB)
                g = mm(ar, wg[b, :, cols], 1, 0)
                u = mm(ar, wu[b, :, cols], 1, 0)
                d = mm(br, wd[b, cols, :], 1, 1).astype(BF).astype(F32)
                s = 1 / (1 + jnp.exp(-g))
                gs = g * s
                hid[rows, cols] = (gs * u).astype(BF)
                dup[rows, cols] = (d * gs).astype(BF)
                dgate[rows, cols] = (d * u * (s + gs * (1 - s))).astype(BF)
        elif w == 4:
            for x in range(2):
                r = mm(hid[:, x * HT : (x + 1) * HT], by[l], 0, 0).astype(BF)
                for q in range(Z):
                    for k in range(DC):
                        full[slot, x, q, OFF_D + k * FR : OFF_D + (k + 1) * FR, :] = r[q * FR : (q + 1) * FR, k * LANES : (k + 1) * LANES]
        elif w in (5, 6):
            src, off = (dgate, 0) if w == 5 else (dup, OFF_U)
            for x in range(2):
                r = mm(a[l], src[:, x * HT : (x + 1) * HT], 0, 0).astype(BF)
                for q in range(Z):
                    for k in range(GC):
                        full[slot, x, q, off + k * DR : off + (k + 1) * DR, :] = r[q * DR : (q + 1) * DR, k * LANES : (k + 1) * LANES]
        else:
            rows = pl.ds((w - 7) * (T // 2), T // 2)

            def by_a():
                return mm(dgate[rows, :], wg[b], 1, 1) + mm(dup[rows, :], wu[b], 1, 1)

            @pl.when((l > 0) & (f == 0))
            def _():
                da[rows, :] = by_a()

            @pl.when((l > 0) & (f > 0))
            def _():
                da[rows, :] += by_a()

            if w == 8:

                @pl.when((l > 0) & (f == NT - 1))
                def _():
                    def of(rows):
                        wide = h[l, rows, :].astype(F32)
                        ct = da[rows, :].astype(BF).astype(F32)
                        scale = lax.rsqrt(jnp.mean(wide * wide, -1, keepdims=True) + 1e-6)
                        by_scale = jnp.sum(ct * wide, -1, keepdims=True)
                        g = ct * scale - wide * (by_scale * (scale * scale * scale) * (1.0 / D))
                        by[l - 1, rows, :] = (by[l, rows, :].astype(F32) + g.astype(BF).astype(F32)).astype(BF)

                    by_rows(128, of)

    def event(j, what, s):
        slot, pb, r = lax.rem(j, NS), lax.rem(j, NP), lax.rem(j, NR)
        swap = pltpu.make_async_remote_copy(
            src_ref=full.at[slot, 1 - c],
            dst_ref=pbuf.at[pb],
            send_sem=d_send.at[pb],
            recv_sem=d_recv.at[pb],
            device_id={"dp": at.mate},
            device_id_type=MESH,
        )

        def send(sums, s, send_sem, recv_sem, to):
            return pltpu.make_async_remote_copy(
                src_ref=sums.at[r, s],
                dst_ref=sums.at[r, s + 1],
                send_sem=send_sem.at[r],
                recv_sem=recv_sem.at[r, s + 1],
                device_id={"dp": to},
                device_id_type=MESH,
            )

        onwards = lambda s: send(on, s, on_send, on_recv, at.next)
        backwards = lambda s: send(back, s, back_send, back_recv, at.prev)

        def own(q):
            q = lax.rem(q + 2 * Z, Z)
            return full[slot, c, q].astype(F32) + pbuf[pb, q].astype(F32)

        if what == "give":
            swap.start()
        elif what == "on":
            if s:
                onwards(s - 1).wait_recv()
                onwards(s - 1).wait_send()
            else:
                swap.wait_recv()
                swap.wait_send()
            total = own(p + UP - s)
            on[r, s] = (total + on[r, s].astype(F32) if s else total).astype(BF)
            onwards(s).start()
        elif what == "back":
            if s:
                backwards(s - 1).wait_recv()
                backwards(s - 1).wait_send()
            total = own(p - DOWN + s)
            back[r, s] = (total + back[r, s].astype(F32) if s else total).astype(BF)
            backwards(s).start()
        else:
            for copy in (onwards(UP - 1), backwards(DOWN - 1)):
                copy.wait_recv()
                copy.wait_send()
            total = (own(p) + on[r, UP].astype(F32) + back[r, DOWN].astype(F32)).astype(BF)
            for k, out in enumerate(outs):

                @pl.when(lax.div(j, NT) == k)
                def _():
                    out[lax.rem(j, NT)] = total

    events = [(0, "give", 0)] + [(STRIDE * (s + 1), "on", s) for s in range(UP)] + [(STRIDE * (s + 1) + LAG, "back", s) for s in range(DOWN)]
    events.append((STRIDE * (UP + 1), "end", 0))

    def macro(i, _):
        for w in range(STEPS):

            @pl.when(i < J)
            def _():
                piece(i, w)

            for wait, what, s in sorted(events, reverse=True):
                if wait % STEPS == w:
                    j = i - 1 - wait // STEPS

                    @pl.when((j >= 0) & (j < J))
                    def _():
                        event(j, what, s)

        return 0

    lax.fori_loop(0, J + 1 + max(events)[0] // STEPS, macro, 0)


def grads(n, x, dy, wg, wu, wd):
    layers, D, FF = wg.shape
    T = x.shape[1]
    Z, HT, NT = n // 2, TILE // 2, FF // TILE
    R = (2 * HT // LANES) * (D // Z) + (D // LANES) * (HT // Z)
    dma, vmem, anywhere = pltpu.SemaphoreType.DMA, pltpu.VMEM, pl.BlockSpec(memory_space=pl.ANY)
    return pl.pallas_call(
        functools.partial(grads_kernel, n, layers),
        out_shape=[jax.ShapeDtypeStruct((NT, R, LANES), BF)] * layers,
        in_specs=[anywhere] * 5,
        out_specs=[pl.BlockSpec(memory_space=pltpu.VMEM)] * layers,
        scratch_shapes=[
            vmem((layers, T, D), BF),
            vmem((layers, T, D), BF),
            vmem((layers, T, D), BF),
            vmem((T, D), F32),
            vmem((2, D, TILE), BF),
            vmem((2, D, TILE), BF),
            vmem((2, TILE, D), BF),
            vmem((T, TILE), BF),
            vmem((T, TILE), BF),
            vmem((T, TILE), BF),
            vmem((NS, 2, Z, R, LANES), BF),
            vmem((NP, Z, R, LANES), BF),
            vmem((NR, Z // 2 + 1, R, LANES), BF),
            vmem((NR, Z - Z // 2, R, LANES), BF),
            dma((2,)),
            dma((2, 2, 3)),
            dma((NP,)),
            dma((NP,)),
            dma((NR,)),
            dma((NR, Z // 2 + 1)),
            dma((NR,)),
            dma((NR, Z - Z // 2)),
        ],
        compiler_params=pltpu.CompilerParams(collective_id=0, has_side_effects=True, vmem_limit_bytes=53 << 20),
        cost_estimate=pl.CostEstimate(flops=2 * T * D * FF * (11 * layers - 5), bytes_accessed=64 << 20, transcendentals=0),
        name="grads",
    )(x, dy, wg, wu, wd)


def adamw(w, m, v, g):
    m = 0.9 * m + 0.1 * g
    v = 0.95 * v + 0.05 * g * g
    step = m * lax.rsqrt(v + 1e-8) + 0.1 * w
    return (w - 0.02 * step).astype(BF), m, v


def update_kernel(n, l, s, sides, unread, *refs):
    terms, refs = refs[: len(sides)], refs[len(sides) :]
    olds, refs = refs[:9], refs[9 + unread :]
    news, (g, *bufs), (g_sem, in_sem, out_sem) = refs[:9], refs[9:19], refs[19:]
    at = Ring(n)
    Z = at.Z
    NT, _, _ = terms[0].shape
    D, FF = olds[0].shape[1:]
    HT = TILE // 2
    DR, FR = D // Z, HT // Z
    GC, DC = HT // LANES, D // LANES
    units, tiles = len(sides) * PARTS, NT // PARTS
    CW = tiles * HT

    def place(arrays, unit):
        side, part = (lax.div(unit, PARTS) if len(sides) > 1 else sides[0]), lax.rem(unit, PARTS)
        q = lax.rem(jnp.where(side == 0, at.p, at.mate_p) + (Z - s), Z)
        half = jnp.where(side == 0, at.c, 1 - at.c)
        rows = pl.ds(pl.multiple_of(q * DR, DR), DR)
        cols = pl.ds(pl.multiple_of(half * (FF // 2) + part * CW, CW), CW)
        return [x.at[l, rows, cols] for x in arrays[:6]] + [x.at[l, half, pl.ds(part * tiles, tiles), q] for x in arrays[6:]]

    def loads(unit):
        return [pltpu.make_async_copy(src, buf.at[unit], in_sem.at[unit, k]) for k, (src, buf) in enumerate(zip(place(olds, unit), bufs, strict=True))]

    def stores(unit):
        return [pltpu.make_async_copy(buf.at[unit], dst, out_sem.at[unit, k]) for k, (dst, buf) in enumerate(zip(place(news, unit), bufs, strict=True))]

    fetched = [pltpu.make_async_copy(terms[0].at[k], g.at[k], g_sem.at[k]) for k in range(NT if 0 in sides else 0)]
    for unit in range(min(AHEAD, units)):
        for copy in (fetched[unit * tiles : (unit + 1) * tiles]) + loads(unit):
            copy.start()

    def one(unit, _):
        for k in range(len(fetched) // tiles):

            @pl.when(unit == k)
            def _():
                for copy in fetched[k * tiles : (k + 1) * tiles]:
                    copy.wait()

        for copy in loads(unit):
            copy.wait()

        @pl.when(unit + AHEAD < units)
        def _():
            for copy in loads(unit + AHEAD):
                copy.start()

        side, part = lax.div(unit, PARTS), lax.rem(unit, PARTS)

        def tile(t, _):
            def step(which, block, index):
                shards = [terms[k] if x else g for k, x in enumerate(sides)]
                grad = shards[0][part * tiles + t, block, :]
                if len(sides) > 1:
                    grad = jnp.where(side == 0, grad, shards[1][part * tiles + t, block, :])
                grad = grad.astype(F32)
                w, m, v = (bufs[3 * which + k] for k in range(3))
                w[index], m[index], v[index] = adamw(w[index].astype(F32), m[index], v[index], grad)

            for which in range(2):
                for k in range(GC):
                    cols = pl.ds(pl.multiple_of(t * HT + k * LANES, LANES), LANES)
                    step(which, pl.ds((which * GC + k) * DR, DR), (unit, slice(None), cols))
            for k in range(DC):
                step(2, pl.ds(2 * GC * DR + k * FR, FR), (unit, t, slice(None), pl.ds(k * LANES, LANES)))
            return 0

        lax.fori_loop(0, tiles, tile, 0)
        for copy in stores(unit):
            copy.start()
        return 0

    lax.fori_loop(0, units, one, 0)

    def end(unit, _):
        for copy in stores(unit):
            copy.wait()
        return 0

    lax.fori_loop(0, units, end, 0)


def update(n, l, s, terms, olds, news):
    sides, terms = tuple(terms), tuple(terms.values())
    NT, R, _ = terms[0].shape
    D, FF = olds[0].shape[1:]
    Z = n // 2
    dma, vmem, anywhere = pltpu.SemaphoreType.DMA, pltpu.VMEM, pl.BlockSpec(memory_space=pl.ANY)
    again = news is not None
    units, size = len(sides) * PARTS, len(sides) * terms[0].size
    wide, tall = (units, D // Z, FF // (2 * PARTS)), (units, NT // PARTS, TILE // 2 // Z, D)
    types = [BF, F32, F32]
    return pl.pallas_call(
        functools.partial(update_kernel, n, l, s, sides, 9 * again),
        out_shape=[jax.ShapeDtypeStruct(x.shape, x.dtype) for x in olds],
        in_specs=[pl.BlockSpec(memory_space=vmem) if x else anywhere for x in sides] + [anywhere] * (9 * (2 if again else 1)),
        out_specs=[anywhere] * 9,
        input_output_aliases={len(sides) + 9 + k: k for k in range(9)} if again else {},
        scratch_shapes=[vmem((NT, R, LANES), BF)]
        + [vmem(wide, t) for t in types] * 2
        + [vmem(tall, t) for t in types]
        + [dma((NT,)), dma((units, 9)), dma((units, 9))],
        compiler_params=pltpu.CompilerParams(vmem_limit_bytes=30 << 20),
        cost_estimate=pl.CostEstimate(flops=4 * 10**9 * len(sides), bytes_accessed=22 * size, transcendentals=size),
        name="update",
    )(*terms, *olds, *(news or ()))


def solution(mesh):
    n = mesh.shape["dp"]
    Z = n // 2
    onward = [(2 * z + c, 2 * ((z + 2 * c - 1) % Z) + c) for z in range(Z) for c in range(2)]
    across = [(2 * z + c, 2 * z + 1 - c) for z in range(Z) for c in range(2)]

    def step(x, dy, *arrays):
        weights, m, v = (arrays[i : i + 3] for i in (0, 3, 6))
        layers, D, FF = weights[0].shape
        NT = FF // TILE
        HT = TILE // 2
        terms = list(grads(n, x, dy, *weights))
        split = (layers, 2, NT, Z, HT // Z, D)
        olds = [y for w in range(3) for y in (weights[w], m[w], v[w])]
        shapes = [y.shape for y in olds]
        olds = olds[:6] + [y.reshape(split) for y in olds[6:]]

        def hop(k):
            return lax.ppermute(terms[k], "dp", onward)

        def swap(k):
            return lax.ppermute(terms[k], "dp", across)

        coming = [hop(k) for k in range(layers)]
        mates = [swap(k) for k in range(layers)]
        news = None
        for s in range(Z):
            for k in range(layers):
                shards = [{0: terms[k], 1: mates[k]}]
                if (k, s) == (layers - 1, Z - 1):
                    shards = [{0: terms[k]}, {1: mates[k]}]
                for part in shards:
                    news = update(n, layers - 1 - k, s, part, olds, news)
                if s < Z - 1:
                    terms[k] = coming[k]
                    if s < Z - 2:
                        coming[k] = hop(k)
                    mates[k] = swap(k)
        news = [y.reshape(shape) for y, shape in zip(news, shapes, strict=True)]
        return tuple(news[3 * w + which] for which in range(3) for w in range(3))

    return jax.shard_map(
        step,
        mesh=mesh,
        in_specs=(P(("rep", "dp"), None, None),) * 2 + (P(None, None, None),) * 9,
        out_specs=(P("rep", None, None),) * 9,
        check_vma=False,
    )
```

profile of v0, /device:TPU:21, one launch (start us, length us, event | category | flops | bytes accessed | tf_op | source)
XLA Modules:
  0.0 407.9 jit_solution(15994440875983695818)
XLA Ops:
  0.7 202.6 %grads.1 = (bf16[8,480,128]{2,1,0:T(8,128)(2,1)}, bf16[8,480,128]{2,1,0:T(8,128)(2,1)}) custom-call(bf16[1,1024,640]{2,1,0:T(8,128)(2,1)} %x_hbm.1, bf16[1,1024,640]{2,1,0:T(8,128)(2,1)} %dy_hbm.1, bf16[2,640,4096]{2,1,0:T(8,128)(2,1)} %refs_1_.3, bf16[2,640,4096]{2,1,0:T(8,128)(2,1)} %refs_4_.33, bf16[2,4096,640]{2,1,0:T(8,128)(2,1)} %wd_hbm.1), custom_call_target="tpu_custom_call" | custom-call | flops 91268055040 | bytes 67108864 | tf_op jit(solution)/shard_map/grads/pallas_call | solution.py:286
  203.9 6.7 %collective-permute-start.29 = (bf16[8,480,128]{2,1,0:T(8,128)(2,1)}, bf16[8,480,128]{2,1,0:T(8,128)(2,1)S(1)}, u32[]{:S(2)}, u32[]{:S(2)}) collective-permute-start(bf16[8,480,128]{2,1,0:T(8,128)(2,1)} %get-tuple-element.165.refs_0_), channel_id=1, source_target_pairs={{0,1},{1,0},{2,3},{3,2},{4,5},{5,4},{6,7},{7,6},{8,9},{9,8},{10,11... | collective-permute-start | bytes 2949128 | tf_op jit(solution)/shard_map/ppermute | solution.py:459
  210.6 7.1 %collective-permute-done.8.refs_0_ = bf16[8,480,128]{2,1,0:T(8,128)(2,1)S(1)} collective-permute-done((bf16[8,480,128]{2,1,0:T(8,128)(2,1)}, bf16[8,480,128]{2,1,0:T(8,128)(2,1)S(1)}, u32[]{:S(2)}, u32[]{:S(2)}) %collective-permute-start.8) | collective-permute-done | bytes 983072 | tf_op jit(solution)/shard_map/ppermute | solution.py:456
  217.7 4.3 %collective-permute-start.27 = (bf16[8,480,128]{2,1,0:T(8,128)(2,1)S(1)}, bf16[8,480,128]{2,1,0:T(8,128)(2,1)S(1)}, u32[]{:S(2)}, u32[]{:S(2)}) collective-permute-start(bf16[8,480,128]{2,1,0:T(8,128)(2,1)S(1)} %collective-permute-done.8.refs_0_), channel_id=1, source_target_pairs={{0,1},{1,0},{2,3},{3,2},{4,5},{5,4},{6,7},{7,6},{8,9},{9,8},{10,11... | collective-permute-start | bytes 2949128 | tf_op jit(solution)/shard_map/ppermute | solution.py:459
  221.9 1.6 collective-permute-start.9
  223.5 4.8 %collective-permute-done.refs_0_ = bf16[8,480,128]{2,1,0:T(8,128)(2,1)} collective-permute-done((bf16[8,480,128]{2,1,0:T(8,128)(2,1)}, bf16[8,480,128]{2,1,0:T(8,128)(2,1)}, u32[]{:S(2)}, u32[]{:S(2)}) %collective-permute-start) | collective-permute-done | bytes 983072 | tf_op jit(solution)/shard_map/ppermute | solution.py:456
  228.3 4.1 %collective-permute-start.26 = (bf16[8,480,128]{2,1,0:T(8,128)(2,1)}, bf16[8,480,128]{2,1,0:T(8,128)(2,1)}, u32[]{:S(2)}, u32[]{:S(2)}) collective-permute-start(bf16[8,480,128]{2,1,0:T(8,128)(2,1)} %collective-permute-done.refs_0_), channel_id=1, source_target_pairs={{0,1},{1,0},{2,3},{3,2},{4,5},{5,4},{6,7},{7,6},{8,9},{9,8},{10,11... | collective-permute-start | bytes 2949128 | tf_op jit(solution)/shard_map/ppermute | solution.py:459
  232.5 1.7 collective-permute-start.1
  234.2 4.0 copy-done.1
  238.2 7.5 %update.17 = (bf16[2,640,4096]{2,1,0:T(8,128)(2,1)}, f32[2,640,4096]{2,1,0:T(8,128)}, f32[2,640,4096]{2,1,0:T(8,128)}, bf16[2,640,4096]{2,1,0:T(8,128)(2,1)}, f3...) custom-call(bf16[8,480,128]{2,1,0:T(8,128)(2,1)} %get-tuple-element., ...), custom_call_target="tpu_custom_call" | custom-call | flops 8000000000 | bytes 21626880 | tf_op jit(solution)/shard_map/update/pallas_call | solution.py:422
  245.6 8.6 %update.18 = (bf16[2,640,4096]{2,1,0:T(8,128)(2,1)}, f32[2,640,4096]{2,1,0:T(8,128)}, f32[2,640,4096]{2,1,0:T(8,128)}, bf16[2,640,4096]{2,1,0:T(8,128)(2,1)}, f3...) custom-call(bf16[8,480,128]{2,1,0:T(8,128)(2,1)S(1)} %copy-done.2, ...), custom_call_target="tpu_custom_call", output_to_operand_aliasing={{0}: (11, {}), {1}: (12, {}), {2}: (13, {}), {3}: (14, {}),... | custom-call | flops 8000000000 | bytes 21626880 | tf_op jit(solution)/shard_map/update/pallas_call | solution.py:422
  254.3 2.1 collective-permute-start.25
  256.9 1.6 collective-permute-start.2
  258.5 8.5 %update.19 = (bf16[2,640,4096]{2,1,0:T(8,128)(2,1)}, f32[2,640,4096]{2,1,0:T(8,128)}, f32[2,640,4096]{2,1,0:T(8,128)}, bf16[2,640,4096]{2,1,0:T(8,128)(2,1)}, f3...) custom-call(bf16[8,480,128]{2,1,0:T(8,128)(2,1)S(1)} %collective-per, ...), custom_call_target="tpu_custom_call", output_to_operand_aliasing={{0}: (11, {}), {1}: (12, {}), {2}: (13, {}), {3}: (14, {}),... | custom-call | flops 8000000000 | bytes 21626880 | tf_op jit(solution)/shard_map/update/pallas_call | solution.py:422
  267.1 8.6 %update.20 = (bf16[2,640,4096]{2,1,0:T(8,128)(2,1)}, f32[2,640,4096]{2,1,0:T(8,128)}, f32[2,640,4096]{2,1,0:T(8,128)}, bf16[2,640,4096]{2,1,0:T(8,128)(2,1)}, f3...) custom-call(bf16[8,480,128]{2,1,0:T(8,128)(2,1)} %collective-permute, ...), custom_call_target="tpu_custom_call", output_to_operand_aliasing={{0}: (11, {}), {1}: (12, {}), {2}: (13, {}), {3}: (14, {}),... | custom-call | flops 8000000000 | bytes 21626880 | tf_op jit(solution)/shard_map/update/pallas_call | solution.py:422
  277.1 4.3 %collective-permute-done.2.refs_0_ = bf16[8,480,128]{2,1,0:T(8,128)(2,1)} collective-permute-done((bf16[8,480,128]{2,1,0:T(8,128)(2,1)}, bf16[8,480,128]{2,1,0:T(8,128)(2,1)}, u32[]{:S(2)}, u32[]{:S(2)}) %collective-permute-start.2) | collective-permute-done | bytes 983072 | tf_op jit(solution)/shard_map/ppermute | solution.py:456
  282.0 8.6 %update.21 = (bf16[2,640,4096]{2,1,0:T(8,128)(2,1)}, f32[2,640,4096]{2,1,0:T(8,128)}, f32[2,640,4096]{2,1,0:T(8,128)}, bf16[2,640,4096]{2,1,0:T(8,128)(2,1)}, f3...) custom-call(bf16[8,480,128]{2,1,0:T(8,128)(2,1)} %collective-permute, ...), custom_call_target="tpu_custom_call", output_to_operand_aliasing={{0}: (11, {}), {1}: (12, {}), {2}: (13, {}), {3}: (14, {}),... | custom-call | flops 8000000000 | bytes 21626880 | tf_op jit(solution)/shard_map/update/pallas_call | solution.py:422
  290.6 8.6 %update.22 = (bf16[2,640,4096]{2,1,0:T(8,128)(2,1)}, f32[2,640,4096]{2,1,0:T(8,128)}, f32[2,640,4096]{2,1,0:T(8,128)}, bf16[2,640,4096]{2,1,0:T(8,128)(2,1)}, f3...) custom-call(bf16[8,480,128]{2,1,0:T(8,128)(2,1)} %collective-permute, ...), custom_call_target="tpu_custom_call", output_to_operand_aliasing={{0}: (11, {}), {1}: (12, {}), {2}: (13, {}), {3}: (14, {}),... | custom-call | flops 8000000000 | bytes 21626880 | tf_op jit(solution)/shard_map/update/pallas_call | solution.py:422
  303.0 8.6 %update.23 = (bf16[2,640,4096]{2,1,0:T(8,128)(2,1)}, f32[2,640,4096]{2,1,0:T(8,128)}, f32[2,640,4096]{2,1,0:T(8,128)}, bf16[2,640,4096]{2,1,0:T(8,128)(2,1)}, f3...) custom-call(bf16[8,480,128]{2,1,0:T(8,128)(2,1)} %collective-permute, ...), custom_call_target="tpu_custom_call", output_to_operand_aliasing={{0}: (11, {}), {1}: (12, {}), {2}: (13, {}), {3}: (14, {}),... | custom-call | flops 8000000000 | bytes 21626880 | tf_op jit(solution)/shard_map/update/pallas_call | solution.py:422
  311.6 8.6 %update.24 = (bf16[2,640,4096]{2,1,0:T(8,128)(2,1)}, f32[2,640,4096]{2,1,0:T(8,128)}, f32[2,640,4096]{2,1,0:T(8,128)}, bf16[2,640,4096]{2,1,0:T(8,128)(2,1)}, f3...) custom-call(bf16[8,480,128]{2,1,0:T(8,128)(2,1)} %collective-permute, ...), custom_call_target="tpu_custom_call", output_to_operand_aliasing={{0}: (11, {}), {1}: (12, {}), {2}: (13, {}), {3}: (14, {}),... | custom-call | flops 8000000000 | bytes 21626880 | tf_op jit(solution)/shard_map/update/pallas_call | solution.py:422
  322.2 3.2 collective-permute-done.4.refs_0_
  326.5 8.6 %update.25 = (bf16[2,640,4096]{2,1,0:T(8,128)(2,1)}, f32[2,640,4096]{2,1,0:T(8,128)}, f32[2,640,4096]{2,1,0:T(8,128)}, bf16[2,640,4096]{2,1,0:T(8,128)(2,1)}, f3...) custom-call(bf16[8,480,128]{2,1,0:T(8,128)(2,1)} %collective-permute, ...), custom_call_target="tpu_custom_call", output_to_operand_aliasing={{0}: (11, {}), {1}: (12, {}), {2}: (13, {}), {3}: (14, {}),... | custom-call | flops 8000000000 | bytes 21626880 | tf_op jit(solution)/shard_map/update/pallas_call | solution.py:422
  335.0 8.6 %update.26 = (bf16[2,640,4096]{2,1,0:T(8,128)(2,1)}, f32[2,640,4096]{2,1,0:T(8,128)}, f32[2,640,4096]{2,1,0:T(8,128)}, bf16[2,640,4096]{2,1,0:T(8,128)(2,1)}, f3...) custom-call(bf16[8,480,128]{2,1,0:T(8,128)(2,1)} %collective-permute, ...), custom_call_target="tpu_custom_call", output_to_operand_aliasing={{0}: (11, {}), {1}: (12, {}), {2}: (13, {}), {3}: (14, {}),... | custom-call | flops 8000000000 | bytes 21626880 | tf_op jit(solution)/shard_map/update/pallas_call | solution.py:422
  343.6 2.0 collective-permute-start.17
  348.0 8.6 %update.27 = (bf16[2,640,4096]{2,1,0:T(8,128)(2,1)}, f32[2,640,4096]{2,1,0:T(8,128)}, f32[2,640,4096]{2,1,0:T(8,128)}, bf16[2,640,4096]{2,1,0:T(8,128)(2,1)}, f3...) custom-call(bf16[8,480,128]{2,1,0:T(8,128)(2,1)} %collective-permute, ...), custom_call_target="tpu_custom_call", output_to_operand_aliasing={{0}: (11, {}), {1}: (12, {}), {2}: (13, {}), {3}: (14, {}),... | custom-call | flops 8000000000 | bytes 21626880 | tf_op jit(solution)/shard_map/update/pallas_call | solution.py:422
  356.5 8.6 %update.28 = (bf16[2,640,4096]{2,1,0:T(8,128)(2,1)}, f32[2,640,4096]{2,1,0:T(8,128)}, f32[2,640,4096]{2,1,0:T(8,128)}, bf16[2,640,4096]{2,1,0:T(8,128)(2,1)}, f3...) custom-call(bf16[8,480,128]{2,1,0:T(8,128)(2,1)} %collective-permute, ...), custom_call_target="tpu_custom_call", output_to_operand_aliasing={{0}: (11, {}), {1}: (12, {}), {2}: (13, {}), {3}: (14, {}),... | custom-call | flops 8000000000 | bytes 21626880 | tf_op jit(solution)/shard_map/update/pallas_call | solution.py:422
  366.7 3.9 collective-permute-done.6.refs_0_
  370.7 8.6 %update.29 = (bf16[2,640,4096]{2,1,0:T(8,128)(2,1)}, f32[2,640,4096]{2,1,0:T(8,128)}, f32[2,640,4096]{2,1,0:T(8,128)}, bf16[2,640,4096]{2,1,0:T(8,128)(2,1)}, f3...) custom-call(bf16[8,480,128]{2,1,0:T(8,128)(2,1)} %collective-permute, ...), custom_call_target="tpu_custom_call", output_to_operand_aliasing={{0}: (11, {}), {1}: (12, {}), {2}: (13, {}), {3}: (14, {}),... | custom-call | flops 8000000000 | bytes 21626880 | tf_op jit(solution)/shard_map/update/pallas_call | solution.py:422
  379.3 8.6 %update.30 = (bf16[2,640,4096]{2,1,0:T(8,128)(2,1)}, f32[2,640,4096]{2,1,0:T(8,128)}, f32[2,640,4096]{2,1,0:T(8,128)}, bf16[2,640,4096]{2,1,0:T(8,128)(2,1)}, f3...) custom-call(bf16[8,480,128]{2,1,0:T(8,128)(2,1)} %collective-permute, ...), custom_call_target="tpu_custom_call", output_to_operand_aliasing={{0}: (11, {}), {1}: (12, {}), {2}: (13, {}), {3}: (14, {}),... | custom-call | flops 8000000000 | bytes 21626880 | tf_op jit(solution)/shard_map/update/pallas_call | solution.py:422
  387.9 8.6 %update.31 = (bf16[2,640,4096]{2,1,0:T(8,128)(2,1)}, f32[2,640,4096]{2,1,0:T(8,128)}, f32[2,640,4096]{2,1,0:T(8,128)}, bf16[2,640,4096]{2,1,0:T(8,128)(2,1)}, f3...) custom-call(bf16[8,480,128]{2,1,0:T(8,128)(2,1)} %collective-permute, ...), custom_call_target="tpu_custom_call", output_to_operand_aliasing={{0}: (11, {}), {1}: (12, {}), {2}: (13, {}), {3}: (14, {}),... | custom-call | flops 8000000000 | bytes 21626880 | tf_op jit(solution)/shard_map/update/pallas_call | solution.py:422
  396.5 5.2 %update.32 = (bf16[2,640,4096]{2,1,0:T(8,128)(2,1)}, f32[2,640,4096]{2,1,0:T(8,128)}, f32[2,640,4096]{2,1,0:T(8,128)}, bf16[2,640,4096]{2,1,0:T(8,128)(2,1)}, f3...) custom-call(bf16[8,480,128]{2,1,0:T(8,128)(2,1)} %collective-permute, ...), custom_call_target="tpu_custom_call", output_to_operand_aliasing={{0}: (10, {}), {1}: (11, {}), {2}: (12, {}), {3}: (13, {}),... | custom-call | flops 4000000000 | bytes 10813440 | tf_op jit(solution)/shard_map/update/pallas_call | solution.py:422
  401.7 6.0 %update.33 = (bf16[2,640,4096]{2,1,0:T(8,128)(2,1)}, f32[2,640,4096]{2,1,0:T(8,128)}, f32[2,640,4096]{2,1,0:T(8,128)}, bf16[2,640,4096]{2,1,0:T(8,128)(2,1)}, f3...) custom-call(bf16[8,480,128]{2,1,0:T(8,128)(2,1)} %collective-permute, ...), custom_call_target="tpu_custom_call", output_to_operand_aliasing={{0}: (10, {}), {1}: (11, {}), {2}: (12, {}), {3}: (13, {}),... | custom-call | flops 4000000000 | bytes 10813440 | tf_op jit(solution)/shard_map/update/pallas_call | solution.py:422
  (52 shorter events, 14.3 us)
Async XLA Ops:
  0.6 233.5 %copy-start = (bf16[2,640,4096]{2,1,0:T(8,128)(2,1)S(1)}, bf16[2,640,4096]{2,1,0:T(8,128)(2,1)}, u32[]{:S(2)}) copy-start(bf16[2,640,4096]{2,1,0:T(8,128)(2,1)} %refs_1_.3) | copy-start | bytes 31457284
  203.2 14.5 %collective-permute-start.8 = (bf16[8,480,128]{2,1,0:T(8,128)(2,1)}, bf16[8,480,128]{2,1,0:T(8,128)(2,1)S(1)}, u32[]{:S(2)}, u32[]{:S(2)}) collective-permute-start(bf16[8,480,128]{2,1,0:T(8,128)(2,1)} %get-tuple-element.165.refs_0_), channel_id=1, source_target_pairs={{0,14},{1,3},{2,0},{3,5},{4,2},{5,7},{6,4},{7,9},{8,6},{9,11},{10,... | collective-permute-start | bytes 2949128 | tf_op jit(solution)/shard_map/ppermute | solution.py:456
  203.8 24.5 %collective-permute-start = (bf16[8,480,128]{2,1,0:T(8,128)(2,1)}, bf16[8,480,128]{2,1,0:T(8,128)(2,1)}, u32[]{:S(2)}, u32[]{:S(2)}) collective-permute-start(bf16[8,480,128]{2,1,0:T(8,128)(2,1)} %get-tuple-element.164.refs_0_), channel_id=1, source_target_pairs={{0,14},{1,3},{2,0},{3,5},{4,2},{5,7},{6,4},{7,9},{8,6},{9,11},{10,... | collective-permute-start | bytes 2949128 | tf_op jit(solution)/shard_map/ppermute | solution.py:456
  203.9 28.6 %collective-permute-start.29 = (bf16[8,480,128]{2,1,0:T(8,128)(2,1)}, bf16[8,480,128]{2,1,0:T(8,128)(2,1)S(1)}, u32[]{:S(2)}, u32[]{:S(2)}) collective-permute-start(bf16[8,480,128]{2,1,0:T(8,128)(2,1)} %get-tuple-element.165.refs_0_), channel_id=1, source_target_pairs={{0,1},{1,0},{2,3},{3,2},{4,5},{5,4},{6,7},{7,6},{8,9},{9,8},{10,11... | collective-permute-start | bytes 2949128 | tf_op jit(solution)/shard_map/ppermute | solution.py:459
  210.6 35.0 %collective-permute-start.28 = (bf16[8,480,128]{2,1,0:T(8,128)(2,1)}, bf16[8,480,128]{2,1,0:T(8,128)(2,1)S(1)}, u32[]{:S(2)}, u32[]{:S(2)}) collective-permute-start(bf16[8,480,128]{2,1,0:T(8,128)(2,1)} %get-tuple-element.164.refs_0_), channel_id=1, source_target_pairs={{0,1},{1,0},{2,3},{3,2},{4,5},{5,4},{6,7},{7,6},{8,9},{9,8},{10,11... | collective-permute-start | bytes 2949128 | tf_op jit(solution)/shard_map/ppermute | solution.py:459
  217.7 39.2 %collective-permute-start.27 = (bf16[8,480,128]{2,1,0:T(8,128)(2,1)S(1)}, bf16[8,480,128]{2,1,0:T(8,128)(2,1)S(1)}, u32[]{:S(2)}, u32[]{:S(2)}) collective-permute-start(bf16[8,480,128]{2,1,0:T(8,128)(2,1)S(1)} %collective-permute-done.8.refs_0_), channel_id=1, source_target_pairs={{0,1},{1,0},{2,3},{3,2},{4,5},{5,4},{6,7},{7,6},{8,9},{9,8},{10,11... | collective-permute-start | bytes 2949128 | tf_op jit(solution)/shard_map/ppermute | solution.py:459
  221.9 32.3 %collective-permute-start.9 = (bf16[8,480,128]{2,1,0:T(8,128)(2,1)S(1)}, bf16[8,480,128]{2,1,0:T(8,128)(2,1)}, u32[]{:S(2)}, u32[]{:S(2)}) collective-permute-start(bf16[8,480,128]{2,1,0:T(8,128)(2,1)S(1)} %collective-permute-done.8.refs_0_), channel_id=1, source_target_pairs={{0,14},{1,3},{2,0},{3,5},{4,2},{5,7},{6,4},{7,9},{8,6},{9,11},{10,... | collective-permute-start | bytes 2949128 | tf_op jit(solution)/shard_map/ppermute | solution.py:456
  228.3 38.7 %collective-permute-start.26 = (bf16[8,480,128]{2,1,0:T(8,128)(2,1)}, bf16[8,480,128]{2,1,0:T(8,128)(2,1)}, u32[]{:S(2)}, u32[]{:S(2)}) collective-permute-start(bf16[8,480,128]{2,1,0:T(8,128)(2,1)} %collective-permute-done.refs_0_), channel_id=1, source_target_pairs={{0,1},{1,0},{2,3},{3,2},{4,5},{5,4},{6,7},{7,6},{8,9},{9,8},{10,11... | collective-permute-start | bytes 2949128 | tf_op jit(solution)/shard_map/ppermute | solution.py:459
  232.5 23.9 %collective-permute-start.1 = (bf16[8,480,128]{2,1,0:T(8,128)(2,1)}, bf16[8,480,128]{2,1,0:T(8,128)(2,1)}, u32[]{:S(2)}, u32[]{:S(2)}) collective-permute-start(bf16[8,480,128]{2,1,0:T(8,128)(2,1)} %collective-permute-done.refs_0_), channel_id=1, source_target_pairs={{0,14},{1,3},{2,0},{3,5},{4,2},{5,7},{6,4},{7,9},{8,6},{9,11},{10,... | collective-permute-start | bytes 2949128 | tf_op jit(solution)/shard_map/ppermute | solution.py:456
  238.2 7.5 %copy-start.2 = (bf16[8,480,128]{2,1,0:T(8,128)(2,1)S(1)}, bf16[8,480,128]{2,1,0:T(8,128)(2,1)}, u32[]{:S(2)}) copy-start(bf16[8,480,128]{2,1,0:T(8,128)(2,1)} %get-tuple-element.164.refs_0_) | copy-start | bytes 2949124
  254.3 27.2 %collective-permute-start.25 = (bf16[8,480,128]{2,1,0:T(8,128)(2,1)}, bf16[8,480,128]{2,1,0:T(8,128)(2,1)}, u32[]{:S(2)}, u32[]{:S(2)}) collective-permute-start(bf16[8,480,128]{2,1,0:T(8,128)(2,1)} %collective-permute-done.9.refs_0_), channel_id=1, source_target_pairs={{0,1},{1,0},{2,3},{3,2},{4,5},{5,4},{6,7},{7,6},{8,9},{9,8},{10,11... | collective-permute-start | bytes 2949128 | tf_op jit(solution)/shard_map/ppermute | solution.py:459
  256.4 19.3 %collective-permute-start.10 = (bf16[8,480,128]{2,1,0:T(8,128)(2,1)}, bf16[8,480,128]{2,1,0:T(8,128)(2,1)}, u32[]{:S(2)}, u32[]{:S(2)}) collective-permute-start(bf16[8,480,128]{2,1,0:T(8,128)(2,1)} %collective-permute-done.9.refs_0_), channel_id=1, source_target_pairs={{0,14},{1,3},{2,0},{3,5},{4,2},{5,7},{6,4},{7,9},{8,6},{9,11},{10,... | collective-permute-start | bytes 2949128 | tf_op jit(solution)/shard_map/ppermute | solution.py:456
  256.4 34.2 %collective-permute-start.24 = (bf16[8,480,128]{2,1,0:T(8,128)(2,1)}, bf16[8,480,128]{2,1,0:T(8,128)(2,1)}, u32[]{:S(2)}, u32[]{:S(2)}) collective-permute-start(bf16[8,480,128]{2,1,0:T(8,128)(2,1)} %collective-permute-done.1.refs_0_), channel_id=1, source_target_pairs={{0,1},{1,0},{2,3},{3,2},{4,5},{5,4},{6,7},{7,6},{8,9},{9,8},{10,11... | collective-permute-start | bytes 2949128 | tf_op jit(solution)/shard_map/ppermute | solution.py:459
  256.9 24.5 %collective-permute-start.2 = (bf16[8,480,128]{2,1,0:T(8,128)(2,1)}, bf16[8,480,128]{2,1,0:T(8,128)(2,1)}, u32[]{:S(2)}, u32[]{:S(2)}) collective-permute-start(bf16[8,480,128]{2,1,0:T(8,128)(2,1)} %collective-permute-done.1.refs_0_), channel_id=1, source_target_pairs={{0,14},{1,3},{2,0},{3,5},{4,2},{5,7},{6,4},{7,9},{8,6},{9,11},{10,... | collective-permute-start | bytes 2949128 | tf_op jit(solution)/shard_map/ppermute | solution.py:456
  275.6 26.9 %collective-permute-start.23 = (bf16[8,480,128]{2,1,0:T(8,128)(2,1)}, bf16[8,480,128]{2,1,0:T(8,128)(2,1)}, u32[]{:S(2)}, u32[]{:S(2)}) collective-permute-start(bf16[8,480,128]{2,1,0:T(8,128)(2,1)} %collective-permute-done.10.refs_0_), channel_id=1, source_target_pairs={{0,1},{1,0},{2,3},{3,2},{4,5},{5,4},{6,7},{7,6},{8,9},{9,8},{10,11... | collective-permute-start | bytes 2949128 | tf_op jit(solution)/shard_map/ppermute | solution.py:459
  277.1 22.0 %collective-permute-start.11 = (bf16[8,480,128]{2,1,0:T(8,128)(2,1)}, bf16[8,480,128]{2,1,0:T(8,128)(2,1)}, u32[]{:S(2)}, u32[]{:S(2)}) collective-permute-start(bf16[8,480,128]{2,1,0:T(8,128)(2,1)} %collective-permute-done.10.refs_0_), channel_id=1, source_target_pairs={{0,14},{1,3},{2,0},{3,5},{4,2},{5,7},{6,4},{7,9},{8,6},{9,11},{10,... | collective-permute-start | bytes 2949128 | tf_op jit(solution)/shard_map/ppermute | solution.py:456
  281.4 30.2 %collective-permute-start.22 = (bf16[8,480,128]{2,1,0:T(8,128)(2,1)}, bf16[8,480,128]{2,1,0:T(8,128)(2,1)}, u32[]{:S(2)}, u32[]{:S(2)}) collective-permute-start(bf16[8,480,128]{2,1,0:T(8,128)(2,1)} %collective-permute-done.2.refs_0_), channel_id=1, source_target_pairs={{0,1},{1,0},{2,3},{3,2},{4,5},{5,4},{6,7},{7,6},{8,9},{9,8},{10,11... | collective-permute-start | bytes 2949128 | tf_op jit(solution)/shard_map/ppermute | solution.py:459
  281.5 21.0 %collective-permute-start.3 = (bf16[8,480,128]{2,1,0:T(8,128)(2,1)}, bf16[8,480,128]{2,1,0:T(8,128)(2,1)}, u32[]{:S(2)}, u32[]{:S(2)}) collective-permute-start(bf16[8,480,128]{2,1,0:T(8,128)(2,1)} %collective-permute-done.2.refs_0_), channel_id=1, source_target_pairs={{0,14},{1,3},{2,0},{3,5},{4,2},{5,7},{6,4},{7,9},{8,6},{9,11},{10,... | collective-permute-start | bytes 2949128 | tf_op jit(solution)/shard_map/ppermute | solution.py:456
  299.1 26.3 %collective-permute-start.21 = (bf16[8,480,128]{2,1,0:T(8,128)(2,1)}, bf16[8,480,128]{2,1,0:T(8,128)(2,1)}, u32[]{:S(2)}, u32[]{:S(2)}) collective-permute-start(bf16[8,480,128]{2,1,0:T(8,128)(2,1)} %collective-permute-done.11.refs_0_), channel_id=1, source_target_pairs={{0,1},{1,0},{2,3},{3,2},{4,5},{5,4},{6,7},{7,6},{8,9},{9,8},{10,11... | collective-permute-start | bytes 2949128 | tf_op jit(solution)/shard_map/ppermute | solution.py:459
  300.3 19.9 %collective-permute-start.12 = (bf16[8,480,128]{2,1,0:T(8,128)(2,1)}, bf16[8,480,128]{2,1,0:T(8,128)(2,1)}, u32[]{:S(2)}, u32[]{:S(2)}) collective-permute-start(bf16[8,480,128]{2,1,0:T(8,128)(2,1)} %collective-permute-done.11.refs_0_), channel_id=1, source_target_pairs={{0,14},{1,3},{2,0},{3,5},{4,2},{5,7},{6,4},{7,9},{8,6},{9,11},{10,... | collective-permute-start | bytes 2949128 | tf_op jit(solution)/shard_map/ppermute | solution.py:456
  302.5 32.6 %collective-permute-start.20 = (bf16[8,480,128]{2,1,0:T(8,128)(2,1)}, bf16[8,480,128]{2,1,0:T(8,128)(2,1)}, u32[]{:S(2)}, u32[]{:S(2)}) collective-permute-start(bf16[8,480,128]{2,1,0:T(8,128)(2,1)} %collective-permute-done.3.refs_0_), channel_id=1, source_target_pairs={{0,1},{1,0},{2,3},{3,2},{4,5},{5,4},{6,7},{7,6},{8,9},{9,8},{10,11... | collective-permute-start | bytes 2949128 | tf_op jit(solution)/shard_map/ppermute | solution.py:459
  302.5 22.8 %collective-permute-start.4 = (bf16[8,480,128]{2,1,0:T(8,128)(2,1)}, bf16[8,480,128]{2,1,0:T(8,128)(2,1)}, u32[]{:S(2)}, u32[]{:S(2)}) collective-permute-start(bf16[8,480,128]{2,1,0:T(8,128)(2,1)} %collective-permute-done.3.refs_0_), channel_id=1, source_target_pairs={{0,14},{1,3},{2,0},{3,5},{4,2},{5,7},{6,4},{7,9},{8,6},{9,11},{10,... | collective-permute-start | bytes 2949128 | tf_op jit(solution)/shard_map/ppermute | solution.py:456
  320.2 26.3 %collective-permute-start.19 = (bf16[8,480,128]{2,1,0:T(8,128)(2,1)}, bf16[8,480,128]{2,1,0:T(8,128)(2,1)}, u32[]{:S(2)}, u32[]{:S(2)}) collective-permute-start(bf16[8,480,128]{2,1,0:T(8,128)(2,1)} %collective-permute-done.12.refs_0_), channel_id=1, source_target_pairs={{0,1},{1,0},{2,3},{3,2},{4,5},{5,4},{6,7},{7,6},{8,9},{9,8},{10,11... | collective-permute-start | bytes 2949128 | tf_op jit(solution)/shard_map/ppermute | solution.py:459
  321.4 22.2 %collective-permute-start.13 = (bf16[8,480,128]{2,1,0:T(8,128)(2,1)}, bf16[8,480,128]{2,1,0:T(8,128)(2,1)}, u32[]{:S(2)}, u32[]{:S(2)}) collective-permute-start(bf16[8,480,128]{2,1,0:T(8,128)(2,1)} %collective-permute-done.12.refs_0_), channel_id=1, source_target_pairs={{0,14},{1,3},{2,0},{3,5},{4,2},{5,7},{6,4},{7,9},{8,6},{9,11},{10,... | collective-permute-start | bytes 2949128 | tf_op jit(solution)/shard_map/ppermute | solution.py:456
  325.3 31.2 %collective-permute-start.18 = (bf16[8,480,128]{2,1,0:T(8,128)(2,1)}, bf16[8,480,128]{2,1,0:T(8,128)(2,1)}, u32[]{:S(2)}, u32[]{:S(2)}) collective-permute-start(bf16[8,480,128]{2,1,0:T(8,128)(2,1)} %collective-permute-done.4.refs_0_), channel_id=1, source_target_pairs={{0,1},{1,0},{2,3},{3,2},{4,5},{5,4},{6,7},{7,6},{8,9},{9,8},{10,11... | collective-permute-start | bytes 2949128 | tf_op jit(solution)/shard_map/ppermute | solution.py:459
  325.4 21.0 %collective-permute-start.5 = (bf16[8,480,128]{2,1,0:T(8,128)(2,1)}, bf16[8,480,128]{2,1,0:T(8,128)(2,1)}, u32[]{:S(2)}, u32[]{:S(2)}) collective-permute-start(bf16[8,480,128]{2,1,0:T(8,128)(2,1)} %collective-permute-done.4.refs_0_), channel_id=1, source_target_pairs={{0,14},{1,3},{2,0},{3,5},{4,2},{5,7},{6,4},{7,9},{8,6},{9,11},{10,... | collective-permute-start | bytes 2949128 | tf_op jit(solution)/shard_map/ppermute | solution.py:456
  343.6 27.1 %collective-permute-start.17 = (bf16[8,480,128]{2,1,0:T(8,128)(2,1)}, bf16[8,480,128]{2,1,0:T(8,128)(2,1)}, u32[]{:S(2)}, u32[]{:S(2)}) collective-permute-start(bf16[8,480,128]{2,1,0:T(8,128)(2,1)} %collective-permute-done.13.refs_0_), channel_id=1, source_target_pairs={{0,1},{1,0},{2,3},{3,2},{4,5},{5,4},{6,7},{7,6},{8,9},{9,8},{10,11... | collective-permute-start | bytes 2949128 | tf_op jit(solution)/shard_map/ppermute | solution.py:459
  345.6 19.5 %collective-permute-start.14 = (bf16[8,480,128]{2,1,0:T(8,128)(2,1)}, bf16[8,480,128]{2,1,0:T(8,128)(2,1)}, u32[]{:S(2)}, u32[]{:S(2)}) collective-permute-start(bf16[8,480,128]{2,1,0:T(8,128)(2,1)} %collective-permute-done.13.refs_0_), channel_id=1, source_target_pairs={{0,14},{1,3},{2,0},{3,5},{4,2},{5,7},{6,4},{7,9},{8,6},{9,11},{10,... | collective-permute-start | bytes 2949128 | tf_op jit(solution)/shard_map/ppermute | solution.py:456
  346.4 32.9 %collective-permute-start.16 = (bf16[8,480,128]{2,1,0:T(8,128)(2,1)}, bf16[8,480,128]{2,1,0:T(8,128)(2,1)}, u32[]{:S(2)}, u32[]{:S(2)}) collective-permute-start(bf16[8,480,128]{2,1,0:T(8,128)(2,1)} %collective-permute-done.5.refs_0_), channel_id=1, source_target_pairs={{0,1},{1,0},{2,3},{3,2},{4,5},{5,4},{6,7},{7,6},{8,9},{9,8},{10,11... | collective-permute-start | bytes 2949128 | tf_op jit(solution)/shard_map/ppermute | solution.py:459
  346.5 24.2 %collective-permute-start.6 = (bf16[8,480,128]{2,1,0:T(8,128)(2,1)}, bf16[8,480,128]{2,1,0:T(8,128)(2,1)}, u32[]{:S(2)}, u32[]{:S(2)}) collective-permute-start(bf16[8,480,128]{2,1,0:T(8,128)(2,1)} %collective-permute-done.5.refs_0_), channel_id=1, source_target_pairs={{0,14},{1,3},{2,0},{3,5},{4,2},{5,7},{6,4},{7,9},{8,6},{9,11},{10,... | collective-permute-start | bytes 2949128 | tf_op jit(solution)/shard_map/ppermute | solution.py:456
  365.1 22.7 %collective-permute-start.15 = (bf16[8,480,128]{2,1,0:T(8,128)(2,1)}, bf16[8,480,128]{2,1,0:T(8,128)(2,1)}, u32[]{:S(2)}, u32[]{:S(2)}) collective-permute-start(bf16[8,480,128]{2,1,0:T(8,128)(2,1)} %collective-permute-done.14.refs_0_), channel_id=1, source_target_pairs={{0,1},{1,0},{2,3},{3,2},{4,5},{5,4},{6,7},{7,6},{8,9},{9,8},{10,11... | collective-permute-start | bytes 2949128 | tf_op jit(solution)/shard_map/ppermute | solution.py:459
  370.6 31.0 %collective-permute-start.7 = (bf16[8,480,128]{2,1,0:T(8,128)(2,1)}, bf16[8,480,128]{2,1,0:T(8,128)(2,1)}, u32[]{:S(2)}, u32[]{:S(2)}) collective-permute-start(bf16[8,480,128]{2,1,0:T(8,128)(2,1)} %collective-permute-done.6.refs_0_), channel_id=1, source_target_pairs={{0,1},{1,0},{2,3},{3,2},{4,5},{5,4},{6,7},{7,6},{8,9},{9,8},{10,11... | collective-permute-start | bytes 2949128 | tf_op jit(solution)/shard_map/ppermute | solution.py:459
  (1 other events, 4.0 us)
where the time goes:
time: 409 us; the launch traced here: 408 us
  Pallas kernels  341 us (83%)
  starting transfers between devices  36.2 us (9%)
  waiting for transfers between devices  25.4 us (6%)
    pallas_call x1, Pallas kernels, grads(): pl.pallas_call(functools.partial(grads_kernel, n, layers), out_shape=[jax...  203 us
    pallas_call x17, Pallas kernels, update(): pl.pallas_call(functools.partial(update_kernel, n, l, s, sides, 9 * again...  139 us
    ppermute x16, starting transfers between devices, swap(): return lax.ppermute(terms[k], 'dp', across)  25.4 us
    ppermute x14, waiting for transfers between devices, hop(): return lax.ppermute(terms[k], 'dp', onward)  25.4 us
    ppermute x14, starting transfers between devices, hop(): return lax.ppermute(terms[k], 'dp', onward)  10.7 us
  transfers between devices with their start and end apart: 30, of which 7 were waited for; matrix products, arithmetic and copies ran while one was open for 0% of the time, Pallas kernels for 33%

commit v1 on v0

--- a/solution.py
+++ b/solution.py
@@ -14,6 +14,7 @@
 TILE = 512
 NS, NP, NR = 5, 5, 5
 STEPS, STRIDE, LAG = 9, 6, 3
+GIVE = 9
 PARTS, AHEAD = 2, 4
 
 
@@ -86,12 +87,8 @@
 
         lax.fori_loop(0, T // size, block, 0)
 
-    def norm(l):
-        def of(rows):
-            wide = h[l, rows, :].astype(F32)
-            a[l, rows, :] = (wide * lax.rsqrt(jnp.mean(wide * wide, -1, keepdims=True) + 1e-6)).astype(BF)
-
-        by_rows(128, of)
+    def normed(wide):
+        return (wide * lax.rsqrt(jnp.mean(wide * wide, -1, keepdims=True) + 1e-6)).astype(BF)
 
     x_in = pltpu.make_async_copy(x_hbm.at[0], h.at[0], in_sem.at[0])
     dy_in = pltpu.make_async_copy(dy_hbm.at[0], by.at[layers - 1], in_sem.at[1])
@@ -103,7 +100,11 @@
     for other in (at.next, at.prev, at.mate):
         pl.semaphore_signal(bar, inc=1, device_id={"dp": other}, device_id_type=MESH)
     x_in.wait()
-    norm(0)
+
+    def first(rows):
+        a[0, rows, :] = normed(h[0, rows, :].astype(F32))
+
+    by_rows(128, first)
 
     def forward(t, _):
         l, f, b = lax.div(t, NT), lax.rem(t, NT), lax.rem(t, 2)
@@ -113,23 +114,29 @@
         def _():
             da[...] = jnp.zeros_like(da)
 
-        for w in range(4):
-            rows = pl.ds(w * RC, RC)
-            ar = a[l, rows, :]
-            for nb in range(0, TILE, NB):
-                cols = pl.ds(nb, NB)
-                g = mm(ar, wg[b, :, cols], 1, 0)
-                u = mm(ar, wu[b, :, cols], 1, 0)
-                hid[rows, cols] = (g * (1 / (1 + jnp.exp(-g))) * u).astype(BF)
-            da[rows, :] += mm(hid[rows, :], wd[b], 1, 0)
+        blocks = [(pl.ds(w * RC, RC), pl.ds(nb, NB)) for w in range(4) for nb in range(0, TILE, NB)]
+        held = None
+        for k in range(len(blocks) + 1):
+            if k < len(blocks):
+                rows, cols = blocks[k]
+                ar = a[l, rows, :]
+                g, u = mm(ar, wg[b, :, cols], 1, 0), mm(ar, wu[b, :, cols], 1, 0)
+            if held is not None:
+                g0, u0 = held
+                rows0, cols0 = blocks[k - 1]
+                hid[rows0, cols0] = (g0 * (1 / (1 + jnp.exp(-g0))) * u0).astype(BF)
+                if k % (TILE // NB) == 0:
+                    da[rows0, :] += mm(hid[rows0, :], wd[b], 1, 0)
+            held = (g, u)
 
         @pl.when(f == NT - 1)
         def _():
             def of(rows):
-                h[l + 1, rows, :] = (h[l, rows, :].astype(F32) + da[rows, :].astype(BF).astype(F32)).astype(BF)
+                y = (h[l, rows, :].astype(F32) + da[rows, :].astype(BF).astype(F32)).astype(BF)
+                h[l + 1, rows, :] = y
+                a[l + 1, rows, :] = normed(y.astype(F32))
 
             by_rows(128, of)
-            norm(l + 1)
 
         return 0
 
@@ -254,8 +261,8 @@
                 def _():
                     out[lax.rem(j, NT)] = total
 
-    events = [(0, "give", 0)] + [(STRIDE * (s + 1), "on", s) for s in range(UP)] + [(STRIDE * (s + 1) + LAG, "back", s) for s in range(DOWN)]
-    events.append((STRIDE * (UP + 1), "end", 0))
+    events = [(GIVE, "give", 0)] + [(STEPS + STRIDE * (s + 1), "on", s) for s in range(UP)] + [(STEPS + STRIDE * (s + 1) + LAG, "back", s) for s in range(DOWN)]
+    events.append((STEPS + STRIDE * (UP + 1), "end", 0))
 
     def macro(i, _):
         for w in range(STEPS):
@@ -266,7 +273,7 @@
 
             for wait, what, s in sorted(events, reverse=True):
                 if wait % STEPS == w:
-                    j = i - 1 - wait // STEPS
+                    j = i - wait // STEPS
 
                     @pl.when((j >= 0) & (j < J))
                     def _():
@@ -274,7 +281,7 @@
 
         return 0
 
-    lax.fori_loop(0, J + 1 + max(events)[0] // STEPS, macro, 0)
+    lax.fori_loop(0, J + max(events)[0] // STEPS, macro, 0)
 
 
 def grads(n, x, dy, wg, wu, wd):
@@ -325,7 +332,7 @@
     return (w - 0.02 * step).astype(BF), m, v
 
 
-def update_kernel(n, l, s, sides, unread, *refs):
+def update_kernel(n, l, s, sides, fetch, unread, *refs):
     terms, refs = refs[: len(sides)], refs[len(sides) :]
     olds, refs = refs[:9], refs[9 + unread :]
     news, (g, *bufs), (g_sem, in_sem, out_sem) = refs[:9], refs[9:19], refs[19:]
@@ -353,7 +360,7 @@
     def stores(unit):
         return [pltpu.make_async_copy(buf.at[unit], dst, out_sem.at[unit, k]) for k, (dst, buf) in enumerate(zip(place(news, unit), bufs, strict=True))]
 
-    fetched = [pltpu.make_async_copy(terms[0].at[k], g.at[k], g_sem.at[k]) for k in range(NT if 0 in sides else 0)]
+    fetched = [pltpu.make_async_copy(terms[0].at[k], g.at[k], g_sem.at[k]) for k in range(NT if fetch else 0)]
     for unit in range(min(AHEAD, units)):
         for copy in (fetched[unit * tiles : (unit + 1) * tiles]) + loads(unit):
             copy.start()
@@ -378,7 +385,7 @@
 
         def tile(t, _):
             def step(which, block, index):
-                shards = [terms[k] if x else g for k, x in enumerate(sides)]
+                shards = [g, *terms[1:]] if fetch else terms
                 grad = shards[0][part * tiles + t, block, :]
                 if len(sides) > 1:
                     grad = jnp.where(side == 0, grad, shards[1][part * tiles + t, block, :])
@@ -411,6 +418,7 @@
 
 def update(n, l, s, terms, olds, news):
     sides, terms = tuple(terms), tuple(terms.values())
+    fetch = sides[0] == 0 and 0 < s < n // 2 - 1
     NT, R, _ = terms[0].shape
     D, FF = olds[0].shape[1:]
     Z = n // 2
@@ -420,9 +428,9 @@
     wide, tall = (units, D // Z, FF // (2 * PARTS)), (units, NT // PARTS, TILE // 2 // Z, D)
     types = [BF, F32, F32]
     return pl.pallas_call(
-        functools.partial(update_kernel, n, l, s, sides, 9 * again),
+        functools.partial(update_kernel, n, l, s, sides, fetch, 9 * again),
         out_shape=[jax.ShapeDtypeStruct(x.shape, x.dtype) for x in olds],
-        in_specs=[pl.BlockSpec(memory_space=vmem) if x else anywhere for x in sides] + [anywhere] * (9 * (2 if again else 1)),
+        in_specs=[anywhere if fetch and x == 0 else pl.BlockSpec(memory_space=vmem) for x in sides] + [anywhere] * (9 * (2 if again else 1)),
         out_specs=[anywhere] * 9,
         input_output_aliases={len(sides) + 9 + k: k for k in range(9)} if again else {},
         scratch_shapes=[vmem((NT, R, LANES), BF)]

time: 409 us -> 409 us (level)
  transfers between devices with their start and end apart: 30 -> 30, of which waited for: 7 -> 7; matrix products, arithmetic and copies ran while one was open for 0% -> 0% of each run, Pallas kernels for 33% -> 32%
where the time goes in v1:
time: 409 us; the launch traced here: 408 us
  Pallas kernels  341 us (83%)
  starting transfers between devices  37.2 us (9%)
  waiting for transfers between devices  25 us (6%)
    pallas_call x1, Pallas kernels, grads(): pl.pallas_call(functools.partial(grads_kernel, n, layers), out_shape=[jax...  202 us
    pallas_call x17, Pallas kernels, update(): pl.pallas_call(functools.partial(update_kernel, n, l, s, sides, fetch, 9...  139 us
    ppermute x16, starting transfers between devices, swap(): return lax.ppermute(terms[k], 'dp', across)  28.9 us
    ppermute x14, waiting for transfers between devices, hop(): return lax.ppermute(terms[k], 'dp', onward)  25 us
    ppermute x14, starting transfers between devices, hop(): return lax.ppermute(terms[k], 'dp', onward)  8.21 us
  transfers between devices with their start and end apart: 30, of which 7 were waited for; matrix products, arithmetic and copies ran while one was open for 0% of the time, Pallas kernels for 32%

profile of v1, /device:TPU:21, one launch (start us, length us, event | category | flops | bytes accessed | tf_op | source)
XLA Modules:
  0.0 408.3 jit_solution(4511858478954150280)
XLA Ops:
  0.7 202.4 %grads.1 = (bf16[8,480,128]{2,1,0:T(8,128)(2,1)}, bf16[8,480,128]{2,1,0:T(8,128)(2,1)}) custom-call(bf16[1,1024,640]{2,1,0:T(8,128)(2,1)} %x_hbm.1, bf16[1,1024,640]{2,1,0:T(8,128)(2,1)} %dy_hbm.1, bf16[2,640,4096]{2,1,0:T(8,128)(2,1)} %refs_1_.3, bf16[2,640,4096]{2,1,0:T(8,128)(2,1)} %refs_4_.33, bf16[2,4096,640]{2,1,0:T(8,128)(2,1)} %wd_hbm.1), custom_call_target="tpu_custom_call" | custom-call | flops 91268055040 | bytes 67108864 | tf_op jit(solution)/shard_map/grads/pallas_call | solution.py:293
  203.7 6.8 %collective-permute-start.29 = (bf16[8,480,128]{2,1,0:T(8,128)(2,1)}, bf16[8,480,128]{2,1,0:T(8,128)(2,1)S(1)}, u32[]{:S(2)}, u32[]{:S(2)}) collective-permute-start(bf16[8,480,128]{2,1,0:T(8,128)(2,1)} %get-tuple-element.165.refs_0_), channel_id=1, source_target_pairs={{0,1},{1,0},{2,3},{3,2},{4,5},{5,4},{6,7},{7,6},{8,9},{9,8},{10,11... | collective-permute-start | bytes 2949128 | tf_op jit(solution)/shard_map/ppermute | solution.py:467
  210.6 6.9 %collective-permute-done.8.refs_0_ = bf16[8,480,128]{2,1,0:T(8,128)(2,1)S(1)} collective-permute-done((bf16[8,480,128]{2,1,0:T(8,128)(2,1)}, bf16[8,480,128]{2,1,0:T(8,128)(2,1)S(1)}, u32[]{:S(2)}, u32[]{:S(2)}) %collective-permute-start.8) | collective-permute-done | bytes 983072 | tf_op jit(solution)/shard_map/ppermute | solution.py:464
  217.5 4.9 %collective-permute-start.27 = (bf16[8,480,128]{2,1,0:T(8,128)(2,1)S(1)}, bf16[8,480,128]{2,1,0:T(8,128)(2,1)S(1)}, u32[]{:S(2)}, u32[]{:S(2)}) collective-permute-start(bf16[8,480,128]{2,1,0:T(8,128)(2,1)S(1)} %collective-permute-done.8.refs_0_), channel_id=1, source_target_pairs={{0,1},{1,0},{2,3},{3,2},{4,5},{5,4},{6,7},{7,6},{8,9},{9,8},{10,11... | collective-permute-start | bytes 2949128 | tf_op jit(solution)/shard_map/ppermute | solution.py:467
  223.9 4.2 %collective-permute-done.refs_0_ = bf16[8,480,128]{2,1,0:T(8,128)(2,1)} collective-permute-done((bf16[8,480,128]{2,1,0:T(8,128)(2,1)}, bf16[8,480,128]{2,1,0:T(8,128)(2,1)}, u32[]{:S(2)}, u32[]{:S(2)}) %collective-permute-start) | collective-permute-done | bytes 983072 | tf_op jit(solution)/shard_map/ppermute | solution.py:464
  228.2 4.8 %collective-permute-start.26 = (bf16[8,480,128]{2,1,0:T(8,128)(2,1)}, bf16[8,480,128]{2,1,0:T(8,128)(2,1)}, u32[]{:S(2)}, u32[]{:S(2)}) collective-permute-start(bf16[8,480,128]{2,1,0:T(8,128)(2,1)} %collective-permute-done.refs_0_), channel_id=1, source_target_pairs={{0,1},{1,0},{2,3},{3,2},{4,5},{5,4},{6,7},{7,6},{8,9},{9,8},{10,11... | collective-permute-start | bytes 2949128 | tf_op jit(solution)/shard_map/ppermute | solution.py:467
  232.9 1.7 collective-permute-start.1
  234.6 4.0 copy-done.1
  238.6 8.3 %update.17 = (bf16[2,640,4096]{2,1,0:T(8,128)(2,1)}, f32[2,640,4096]{2,1,0:T(8,128)}, f32[2,640,4096]{2,1,0:T(8,128)}, bf16[2,640,4096]{2,1,0:T(8,128)(2,1)}, f3...) custom-call(bf16[8,480,128]{2,1,0:T(8,128)(2,1)} %get-tuple-element., ...), custom_call_target="tpu_custom_call" | custom-call | flops 8000000000 | bytes 21626880 | tf_op jit(solution)/shard_map/update/pallas_call | solution.py:430
  246.9 7.0 %update.18 = (bf16[2,640,4096]{2,1,0:T(8,128)(2,1)}, f32[2,640,4096]{2,1,0:T(8,128)}, f32[2,640,4096]{2,1,0:T(8,128)}, bf16[2,640,4096]{2,1,0:T(8,128)(2,1)}, f3...) custom-call(bf16[8,480,128]{2,1,0:T(8,128)(2,1)S(1)} %copy-done.2, ...), custom_call_target="tpu_custom_call", output_to_operand_aliasing={{0}: (11, {}), {1}: (12, {}), {2}: (13, {}), {3}: (14, {}),... | custom-call | flops 8000000000 | bytes 21626880 | tf_op jit(solution)/shard_map/update/pallas_call | solution.py:430
  253.9 2.1 collective-permute-start.25
  257.9 8.5 %update.19 = (bf16[2,640,4096]{2,1,0:T(8,128)(2,1)}, f32[2,640,4096]{2,1,0:T(8,128)}, f32[2,640,4096]{2,1,0:T(8,128)}, bf16[2,640,4096]{2,1,0:T(8,128)(2,1)}, f3...) custom-call(bf16[8,480,128]{2,1,0:T(8,128)(2,1)S(1)} %collective-per, ...), custom_call_target="tpu_custom_call", output_to_operand_aliasing={{0}: (11, {}), {1}: (12, {}), {2}: (13, {}), {3}: (14, {}),... | custom-call | flops 8000000000 | bytes 21626880 | tf_op jit(solution)/shard_map/update/pallas_call | solution.py:430
  266.5 8.6 %update.20 = (bf16[2,640,4096]{2,1,0:T(8,128)(2,1)}, f32[2,640,4096]{2,1,0:T(8,128)}, f32[2,640,4096]{2,1,0:T(8,128)}, bf16[2,640,4096]{2,1,0:T(8,128)(2,1)}, f3...) custom-call(bf16[8,480,128]{2,1,0:T(8,128)(2,1)} %collective-permute, ...), custom_call_target="tpu_custom_call", output_to_operand_aliasing={{0}: (11, {}), {1}: (12, {}), {2}: (13, {}), {3}: (14, {}),... | custom-call | flops 8000000000 | bytes 21626880 | tf_op jit(solution)/shard_map/update/pallas_call | solution.py:430
  275.1 1.7 collective-permute-start.23
  276.8 4.3 %collective-permute-done.2.refs_0_ = bf16[8,480,128]{2,1,0:T(8,128)(2,1)} collective-permute-done((bf16[8,480,128]{2,1,0:T(8,128)(2,1)}, bf16[8,480,128]{2,1,0:T(8,128)(2,1)}, u32[]{:S(2)}, u32[]{:S(2)}) %collective-permute-start.2) | collective-permute-done | bytes 983072 | tf_op jit(solution)/shard_map/ppermute | solution.py:464
  281.2 8.6 %update.21 = (bf16[2,640,4096]{2,1,0:T(8,128)(2,1)}, f32[2,640,4096]{2,1,0:T(8,128)}, f32[2,640,4096]{2,1,0:T(8,128)}, bf16[2,640,4096]{2,1,0:T(8,128)(2,1)}, f3...) custom-call(bf16[8,480,128]{2,1,0:T(8,128)(2,1)} %collective-permute, ...), custom_call_target="tpu_custom_call", output_to_operand_aliasing={{0}: (11, {}), {1}: (12, {}), {2}: (13, {}), {3}: (14, {}),... | custom-call | flops 8000000000 | bytes 21626880 | tf_op jit(solution)/shard_map/update/pallas_call | solution.py:430
  289.8 8.6 %update.22 = (bf16[2,640,4096]{2,1,0:T(8,128)(2,1)}, f32[2,640,4096]{2,1,0:T(8,128)}, f32[2,640,4096]{2,1,0:T(8,128)}, bf16[2,640,4096]{2,1,0:T(8,128)(2,1)}, f3...) custom-call(bf16[8,480,128]{2,1,0:T(8,128)(2,1)} %collective-permute, ...), custom_call_target="tpu_custom_call", output_to_operand_aliasing={{0}: (11, {}), {1}: (12, {}), {2}: (13, {}), {3}: (14, {}),... | custom-call | flops 8000000000 | bytes 21626880 | tf_op jit(solution)/shard_map/update/pallas_call | solution.py:430
  302.3 8.6 %update.23 = (bf16[2,640,4096]{2,1,0:T(8,128)(2,1)}, f32[2,640,4096]{2,1,0:T(8,128)}, f32[2,640,4096]{2,1,0:T(8,128)}, bf16[2,640,4096]{2,1,0:T(8,128)(2,1)}, f3...) custom-call(bf16[8,480,128]{2,1,0:T(8,128)(2,1)} %collective-permute, ...), custom_call_target="tpu_custom_call", output_to_operand_aliasing={{0}: (11, {}), {1}: (12, {}), {2}: (13, {}), {3}: (14, {}),... | custom-call | flops 8000000000 | bytes 21626880 | tf_op jit(solution)/shard_map/update/pallas_call | solution.py:430
  310.8 8.6 %update.24 = (bf16[2,640,4096]{2,1,0:T(8,128)(2,1)}, f32[2,640,4096]{2,1,0:T(8,128)}, f32[2,640,4096]{2,1,0:T(8,128)}, bf16[2,640,4096]{2,1,0:T(8,128)(2,1)}, f3...) custom-call(bf16[8,480,128]{2,1,0:T(8,128)(2,1)} %collective-permute, ...), custom_call_target="tpu_custom_call", output_to_operand_aliasing={{0}: (11, {}), {1}: (12, {}), {2}: (13, {}), {3}: (14, {}),... | custom-call | flops 8000000000 | bytes 21626880 | tf_op jit(solution)/shard_map/update/pallas_call | solution.py:430
  321.7 3.4 collective-permute-done.4.refs_0_
  325.7 8.6 %update.25 = (bf16[2,640,4096]{2,1,0:T(8,128)(2,1)}, f32[2,640,4096]{2,1,0:T(8,128)}, f32[2,640,4096]{2,1,0:T(8,128)}, bf16[2,640,4096]{2,1,0:T(8,128)(2,1)}, f3...) custom-call(bf16[8,480,128]{2,1,0:T(8,128)(2,1)} %collective-permute, ...), custom_call_target="tpu_custom_call", output_to_operand_aliasing={{0}: (11, {}), {1}: (12, {}), {2}: (13, {}), {3}: (14, {}),... | custom-call | flops 8000000000 | bytes 21626880 | tf_op jit(solution)/shard_map/update/pallas_call | solution.py:430
  334.2 8.6 %update.26 = (bf16[2,640,4096]{2,1,0:T(8,128)(2,1)}, f32[2,640,4096]{2,1,0:T(8,128)}, f32[2,640,4096]{2,1,0:T(8,128)}, bf16[2,640,4096]{2,1,0:T(8,128)(2,1)}, f3...) custom-call(bf16[8,480,128]{2,1,0:T(8,128)(2,1)} %collective-permute, ...), custom_call_target="tpu_custom_call", output_to_operand_aliasing={{0}: (11, {}), {1}: (12, {}), {2}: (13, {}), {3}: (14, {}),... | custom-call | flops 8000000000 | bytes 21626880 | tf_op jit(solution)/shard_map/update/pallas_call | solution.py:430
  342.8 2.5 collective-permute-start.17
  347.2 8.6 %update.27 = (bf16[2,640,4096]{2,1,0:T(8,128)(2,1)}, f32[2,640,4096]{2,1,0:T(8,128)}, f32[2,640,4096]{2,1,0:T(8,128)}, bf16[2,640,4096]{2,1,0:T(8,128)(2,1)}, f3...) custom-call(bf16[8,480,128]{2,1,0:T(8,128)(2,1)} %collective-permute, ...), custom_call_target="tpu_custom_call", output_to_operand_aliasing={{0}: (11, {}), {1}: (12, {}), {2}: (13, {}), {3}: (14, {}),... | custom-call | flops 8000000000 | bytes 21626880 | tf_op jit(solution)/shard_map/update/pallas_call | solution.py:430
  355.8 8.6 %update.28 = (bf16[2,640,4096]{2,1,0:T(8,128)(2,1)}, f32[2,640,4096]{2,1,0:T(8,128)}, f32[2,640,4096]{2,1,0:T(8,128)}, bf16[2,640,4096]{2,1,0:T(8,128)(2,1)}, f3...) custom-call(bf16[8,480,128]{2,1,0:T(8,128)(2,1)} %collective-permute, ...), custom_call_target="tpu_custom_call", output_to_operand_aliasing={{0}: (11, {}), {1}: (12, {}), {2}: (13, {}), {3}: (14, {}),... | custom-call | flops 8000000000 | bytes 21626880 | tf_op jit(solution)/shard_map/update/pallas_call | solution.py:430
  364.4 2.0 collective-permute-start.15
  366.4 3.9 collective-permute-done.6.refs_0_
  370.4 8.6 %update.29 = (bf16[2,640,4096]{2,1,0:T(8,128)(2,1)}, f32[2,640,4096]{2,1,0:T(8,128)}, f32[2,640,4096]{2,1,0:T(8,128)}, bf16[2,640,4096]{2,1,0:T(8,128)(2,1)}, f3...) custom-call(bf16[8,480,128]{2,1,0:T(8,128)(2,1)} %collective-permute, ...), custom_call_target="tpu_custom_call", output_to_operand_aliasing={{0}: (11, {}), {1}: (12, {}), {2}: (13, {}), {3}: (14, {}),... | custom-call | flops 8000000000 | bytes 21626880 | tf_op jit(solution)/shard_map/update/pallas_call | solution.py:430
  379.0 8.6 %update.30 = (bf16[2,640,4096]{2,1,0:T(8,128)(2,1)}, f32[2,640,4096]{2,1,0:T(8,128)}, f32[2,640,4096]{2,1,0:T(8,128)}, bf16[2,640,4096]{2,1,0:T(8,128)(2,1)}, f3...) custom-call(bf16[8,480,128]{2,1,0:T(8,128)(2,1)} %collective-permute, ...), custom_call_target="tpu_custom_call", output_to_operand_aliasing={{0}: (11, {}), {1}: (12, {}), {2}: (13, {}), {3}: (14, {}),... | custom-call | flops 8000000000 | bytes 21626880 | tf_op jit(solution)/shard_map/update/pallas_call | solution.py:430
  387.6 8.5 %update.31 = (bf16[2,640,4096]{2,1,0:T(8,128)(2,1)}, f32[2,640,4096]{2,1,0:T(8,128)}, f32[2,640,4096]{2,1,0:T(8,128)}, bf16[2,640,4096]{2,1,0:T(8,128)(2,1)}, f3...) custom-call(bf16[8,480,128]{2,1,0:T(8,128)(2,1)} %collective-permute, ...), custom_call_target="tpu_custom_call", output_to_operand_aliasing={{0}: (11, {}), {1}: (12, {}), {2}: (13, {}), {3}: (14, {}),... | custom-call | flops 8000000000 | bytes 21626880 | tf_op jit(solution)/shard_map/update/pallas_call | solution.py:430
  396.1 6.0 %update.32 = (bf16[2,640,4096]{2,1,0:T(8,128)(2,1)}, f32[2,640,4096]{2,1,0:T(8,128)}, f32[2,640,4096]{2,1,0:T(8,128)}, bf16[2,640,4096]{2,1,0:T(8,128)(2,1)}, f3...) custom-call(bf16[8,480,128]{2,1,0:T(8,128)(2,1)} %collective-permute, ...), custom_call_target="tpu_custom_call", output_to_operand_aliasing={{0}: (10, {}), {1}: (11, {}), {2}: (12, {}), {3}: (13, {}),... | custom-call | flops 4000000000 | bytes 10813440 | tf_op jit(solution)/shard_map/update/pallas_call | solution.py:430
  402.1 6.0 %update.33 = (bf16[2,640,4096]{2,1,0:T(8,128)(2,1)}, f32[2,640,4096]{2,1,0:T(8,128)}, f32[2,640,4096]{2,1,0:T(8,128)}, bf16[2,640,4096]{2,1,0:T(8,128)(2,1)}, f3...) custom-call(bf16[8,480,128]{2,1,0:T(8,128)(2,1)} %collective-permute, ...), custom_call_target="tpu_custom_call", output_to_operand_aliasing={{0}: (10, {}), {1}: (11, {}), {2}: (12, {}), {3}: (13, {}),... | custom-call | flops 4000000000 | bytes 10813440 | tf_op jit(solution)/shard_map/update/pallas_call | solution.py:430
  (52 shorter events, 13.0 us)
Async XLA Ops:
  0.6 233.9 %copy-start = (bf16[2,640,4096]{2,1,0:T(8,128)(2,1)S(1)}, bf16[2,640,4096]{2,1,0:T(8,128)(2,1)}, u32[]{:S(2)}) copy-start(bf16[2,640,4096]{2,1,0:T(8,128)(2,1)} %refs_1_.3) | copy-start | bytes 31457284
  203.1 14.5 %collective-permute-start.8 = (bf16[8,480,128]{2,1,0:T(8,128)(2,1)}, bf16[8,480,128]{2,1,0:T(8,128)(2,1)S(1)}, u32[]{:S(2)}, u32[]{:S(2)}) collective-permute-start(bf16[8,480,128]{2,1,0:T(8,128)(2,1)} %get-tuple-element.165.refs_0_), channel_id=1, source_target_pairs={{0,14},{1,3},{2,0},{3,5},{4,2},{5,7},{6,4},{7,9},{8,6},{9,11},{10,... | collective-permute-start | bytes 2949128 | tf_op jit(solution)/shard_map/ppermute | solution.py:464
  203.2 25.0 %collective-permute-start = (bf16[8,480,128]{2,1,0:T(8,128)(2,1)}, bf16[8,480,128]{2,1,0:T(8,128)(2,1)}, u32[]{:S(2)}, u32[]{:S(2)}) collective-permute-start(bf16[8,480,128]{2,1,0:T(8,128)(2,1)} %get-tuple-element.164.refs_0_), channel_id=1, source_target_pairs={{0,14},{1,3},{2,0},{3,5},{4,2},{5,7},{6,4},{7,9},{8,6},{9,11},{10,... | collective-permute-start | bytes 2949128 | tf_op jit(solution)/shard_map/ppermute | solution.py:464
  203.7 29.2 %collective-permute-start.29 = (bf16[8,480,128]{2,1,0:T(8,128)(2,1)}, bf16[8,480,128]{2,1,0:T(8,128)(2,1)S(1)}, u32[]{:S(2)}, u32[]{:S(2)}) collective-permute-start(bf16[8,480,128]{2,1,0:T(8,128)(2,1)} %get-tuple-element.165.refs_0_), channel_id=1, source_target_pairs={{0,1},{1,0},{2,3},{3,2},{4,5},{5,4},{6,7},{7,6},{8,9},{9,8},{10,11... | collective-permute-start | bytes 2949128 | tf_op jit(solution)/shard_map/ppermute | solution.py:467
  210.6 36.3 %collective-permute-start.28 = (bf16[8,480,128]{2,1,0:T(8,128)(2,1)}, bf16[8,480,128]{2,1,0:T(8,128)(2,1)S(1)}, u32[]{:S(2)}, u32[]{:S(2)}) collective-permute-start(bf16[8,480,128]{2,1,0:T(8,128)(2,1)} %get-tuple-element.164.refs_0_), channel_id=1, source_target_pairs={{0,1},{1,0},{2,3},{3,2},{4,5},{5,4},{6,7},{7,6},{8,9},{9,8},{10,11... | collective-permute-start | bytes 2949128 | tf_op jit(solution)/shard_map/ppermute | solution.py:467
  217.5 39.1 %collective-permute-start.27 = (bf16[8,480,128]{2,1,0:T(8,128)(2,1)S(1)}, bf16[8,480,128]{2,1,0:T(8,128)(2,1)S(1)}, u32[]{:S(2)}, u32[]{:S(2)}) collective-permute-start(bf16[8,480,128]{2,1,0:T(8,128)(2,1)S(1)} %collective-permute-done.8.refs_0_), channel_id=1, source_target_pairs={{0,1},{1,0},{2,3},{3,2},{4,5},{5,4},{6,7},{7,6},{8,9},{9,8},{10,11... | collective-permute-start | bytes 2949128 | tf_op jit(solution)/shard_map/ppermute | solution.py:467
  222.4 31.5 %collective-permute-start.9 = (bf16[8,480,128]{2,1,0:T(8,128)(2,1)S(1)}, bf16[8,480,128]{2,1,0:T(8,128)(2,1)}, u32[]{:S(2)}, u32[]{:S(2)}) collective-permute-start(bf16[8,480,128]{2,1,0:T(8,128)(2,1)S(1)} %collective-permute-done.8.refs_0_), channel_id=1, source_target_pairs={{0,14},{1,3},{2,0},{3,5},{4,2},{5,7},{6,4},{7,9},{8,6},{9,11},{10,... | collective-permute-start | bytes 2949128 | tf_op jit(solution)/shard_map/ppermute | solution.py:464
  228.2 38.3 %collective-permute-start.26 = (bf16[8,480,128]{2,1,0:T(8,128)(2,1)}, bf16[8,480,128]{2,1,0:T(8,128)(2,1)}, u32[]{:S(2)}, u32[]{:S(2)}) collective-permute-start(bf16[8,480,128]{2,1,0:T(8,128)(2,1)} %collective-permute-done.refs_0_), channel_id=1, source_target_pairs={{0,1},{1,0},{2,3},{3,2},{4,5},{5,4},{6,7},{7,6},{8,9},{9,8},{10,11... | collective-permute-start | bytes 2949128 | tf_op jit(solution)/shard_map/ppermute | solution.py:467
  232.9 23.1 %collective-permute-start.1 = (bf16[8,480,128]{2,1,0:T(8,128)(2,1)}, bf16[8,480,128]{2,1,0:T(8,128)(2,1)}, u32[]{:S(2)}, u32[]{:S(2)}) collective-permute-start(bf16[8,480,128]{2,1,0:T(8,128)(2,1)} %collective-permute-done.refs_0_), channel_id=1, source_target_pairs={{0,14},{1,3},{2,0},{3,5},{4,2},{5,7},{6,4},{7,9},{8,6},{9,11},{10,... | collective-permute-start | bytes 2949128 | tf_op jit(solution)/shard_map/ppermute | solution.py:464
  238.6 8.3 %copy-start.2 = (bf16[8,480,128]{2,1,0:T(8,128)(2,1)S(1)}, bf16[8,480,128]{2,1,0:T(8,128)(2,1)}, u32[]{:S(2)}) copy-start(bf16[8,480,128]{2,1,0:T(8,128)(2,1)} %get-tuple-element.164.refs_0_) | copy-start | bytes 2949124
  253.9 27.2 %collective-permute-start.25 = (bf16[8,480,128]{2,1,0:T(8,128)(2,1)}, bf16[8,480,128]{2,1,0:T(8,128)(2,1)}, u32[]{:S(2)}, u32[]{:S(2)}) collective-permute-start(bf16[8,480,128]{2,1,0:T(8,128)(2,1)} %collective-permute-done.9.refs_0_), channel_id=1, source_target_pairs={{0,1},{1,0},{2,3},{3,2},{4,5},{5,4},{6,7},{7,6},{8,9},{9,8},{10,11... | collective-permute-start | bytes 2949128 | tf_op jit(solution)/shard_map/ppermute | solution.py:467
  256.1 19.0 %collective-permute-start.10 = (bf16[8,480,128]{2,1,0:T(8,128)(2,1)}, bf16[8,480,128]{2,1,0:T(8,128)(2,1)}, u32[]{:S(2)}, u32[]{:S(2)}) collective-permute-start(bf16[8,480,128]{2,1,0:T(8,128)(2,1)} %collective-permute-done.9.refs_0_), channel_id=1, source_target_pairs={{0,14},{1,3},{2,0},{3,5},{4,2},{5,7},{6,4},{7,9},{8,6},{9,11},{10,... | collective-permute-start | bytes 2949128 | tf_op jit(solution)/shard_map/ppermute | solution.py:464
  256.1 33.7 %collective-permute-start.24 = (bf16[8,480,128]{2,1,0:T(8,128)(2,1)}, bf16[8,480,128]{2,1,0:T(8,128)(2,1)}, u32[]{:S(2)}, u32[]{:S(2)}) collective-permute-start(bf16[8,480,128]{2,1,0:T(8,128)(2,1)} %collective-permute-done.1.refs_0_), channel_id=1, source_target_pairs={{0,1},{1,0},{2,3},{3,2},{4,5},{5,4},{6,7},{7,6},{8,9},{9,8},{10,11... | collective-permute-start | bytes 2949128 | tf_op jit(solution)/shard_map/ppermute | solution.py:467
  256.6 24.5 %collective-permute-start.2 = (bf16[8,480,128]{2,1,0:T(8,128)(2,1)}, bf16[8,480,128]{2,1,0:T(8,128)(2,1)}, u32[]{:S(2)}, u32[]{:S(2)}) collective-permute-start(bf16[8,480,128]{2,1,0:T(8,128)(2,1)} %collective-permute-done.1.refs_0_), channel_id=1, source_target_pairs={{0,14},{1,3},{2,0},{3,5},{4,2},{5,7},{6,4},{7,9},{8,6},{9,11},{10,... | collective-permute-start | bytes 2949128 | tf_op jit(solution)/shard_map/ppermute | solution.py:464
  275.1 27.1 %collective-permute-start.23 = (bf16[8,480,128]{2,1,0:T(8,128)(2,1)}, bf16[8,480,128]{2,1,0:T(8,128)(2,1)}, u32[]{:S(2)}, u32[]{:S(2)}) collective-permute-start(bf16[8,480,128]{2,1,0:T(8,128)(2,1)} %collective-permute-done.10.refs_0_), channel_id=1, source_target_pairs={{0,1},{1,0},{2,3},{3,2},{4,5},{5,4},{6,7},{7,6},{8,9},{9,8},{10,11... | collective-permute-start | bytes 2949128 | tf_op jit(solution)/shard_map/ppermute | solution.py:467
  276.8 21.6 %collective-permute-start.11 = (bf16[8,480,128]{2,1,0:T(8,128)(2,1)}, bf16[8,480,128]{2,1,0:T(8,128)(2,1)}, u32[]{:S(2)}, u32[]{:S(2)}) collective-permute-start(bf16[8,480,128]{2,1,0:T(8,128)(2,1)} %collective-permute-done.10.refs_0_), channel_id=1, source_target_pairs={{0,14},{1,3},{2,0},{3,5},{4,2},{5,7},{6,4},{7,9},{8,6},{9,11},{10,... | collective-permute-start | bytes 2949128 | tf_op jit(solution)/shard_map/ppermute | solution.py:464
  281.1 29.8 %collective-permute-start.22 = (bf16[8,480,128]{2,1,0:T(8,128)(2,1)}, bf16[8,480,128]{2,1,0:T(8,128)(2,1)}, u32[]{:S(2)}, u32[]{:S(2)}) collective-permute-start(bf16[8,480,128]{2,1,0:T(8,128)(2,1)} %collective-permute-done.2.refs_0_), channel_id=1, source_target_pairs={{0,1},{1,0},{2,3},{3,2},{4,5},{5,4},{6,7},{7,6},{8,9},{9,8},{10,11... | collective-permute-start | bytes 2949128 | tf_op jit(solution)/shard_map/ppermute | solution.py:467
  281.1 21.0 %collective-permute-start.3 = (bf16[8,480,128]{2,1,0:T(8,128)(2,1)}, bf16[8,480,128]{2,1,0:T(8,128)(2,1)}, u32[]{:S(2)}, u32[]{:S(2)}) collective-permute-start(bf16[8,480,128]{2,1,0:T(8,128)(2,1)} %collective-permute-done.2.refs_0_), channel_id=1, source_target_pairs={{0,14},{1,3},{2,0},{3,5},{4,2},{5,7},{6,4},{7,9},{8,6},{9,11},{10,... | collective-permute-start | bytes 2949128 | tf_op jit(solution)/shard_map/ppermute | solution.py:464
  298.4 26.7 %collective-permute-start.21 = (bf16[8,480,128]{2,1,0:T(8,128)(2,1)}, bf16[8,480,128]{2,1,0:T(8,128)(2,1)}, u32[]{:S(2)}, u32[]{:S(2)}) collective-permute-start(bf16[8,480,128]{2,1,0:T(8,128)(2,1)} %collective-permute-done.11.refs_0_), channel_id=1, source_target_pairs={{0,1},{1,0},{2,3},{3,2},{4,5},{5,4},{6,7},{7,6},{8,9},{9,8},{10,11... | collective-permute-start | bytes 2949128 | tf_op jit(solution)/shard_map/ppermute | solution.py:467
  300.0 19.4 %collective-permute-start.12 = (bf16[8,480,128]{2,1,0:T(8,128)(2,1)}, bf16[8,480,128]{2,1,0:T(8,128)(2,1)}, u32[]{:S(2)}, u32[]{:S(2)}) collective-permute-start(bf16[8,480,128]{2,1,0:T(8,128)(2,1)} %collective-permute-done.11.refs_0_), channel_id=1, source_target_pairs={{0,14},{1,3},{2,0},{3,5},{4,2},{5,7},{6,4},{7,9},{8,6},{9,11},{10,... | collective-permute-start | bytes 2949128 | tf_op jit(solution)/shard_map/ppermute | solution.py:464
  302.1 32.1 %collective-permute-start.20 = (bf16[8,480,128]{2,1,0:T(8,128)(2,1)}, bf16[8,480,128]{2,1,0:T(8,128)(2,1)}, u32[]{:S(2)}, u32[]{:S(2)}) collective-permute-start(bf16[8,480,128]{2,1,0:T(8,128)(2,1)} %collective-permute-done.3.refs_0_), channel_id=1, source_target_pairs={{0,1},{1,0},{2,3},{3,2},{4,5},{5,4},{6,7},{7,6},{8,9},{9,8},{10,11... | collective-permute-start | bytes 2949128 | tf_op jit(solution)/shard_map/ppermute | solution.py:467
  302.2 22.8 %collective-permute-start.4 = (bf16[8,480,128]{2,1,0:T(8,128)(2,1)}, bf16[8,480,128]{2,1,0:T(8,128)(2,1)}, u32[]{:S(2)}, u32[]{:S(2)}) collective-permute-start(bf16[8,480,128]{2,1,0:T(8,128)(2,1)} %collective-permute-done.3.refs_0_), channel_id=1, source_target_pairs={{0,14},{1,3},{2,0},{3,5},{4,2},{5,7},{6,4},{7,9},{8,6},{9,11},{10,... | collective-permute-start | bytes 2949128 | tf_op jit(solution)/shard_map/ppermute | solution.py:464
  319.4 26.7 %collective-permute-start.19 = (bf16[8,480,128]{2,1,0:T(8,128)(2,1)}, bf16[8,480,128]{2,1,0:T(8,128)(2,1)}, u32[]{:S(2)}, u32[]{:S(2)}) collective-permute-start(bf16[8,480,128]{2,1,0:T(8,128)(2,1)} %collective-permute-done.12.refs_0_), channel_id=1, source_target_pairs={{0,1},{1,0},{2,3},{3,2},{4,5},{5,4},{6,7},{7,6},{8,9},{9,8},{10,11... | collective-permute-start | bytes 2949128 | tf_op jit(solution)/shard_map/ppermute | solution.py:467
  321.1 21.8 %collective-permute-start.13 = (bf16[8,480,128]{2,1,0:T(8,128)(2,1)}, bf16[8,480,128]{2,1,0:T(8,128)(2,1)}, u32[]{:S(2)}, u32[]{:S(2)}) collective-permute-start(bf16[8,480,128]{2,1,0:T(8,128)(2,1)} %collective-permute-done.12.refs_0_), channel_id=1, source_target_pairs={{0,14},{1,3},{2,0},{3,5},{4,2},{5,7},{6,4},{7,9},{8,6},{9,11},{10,... | collective-permute-start | bytes 2949128 | tf_op jit(solution)/shard_map/ppermute | solution.py:464
  325.0 30.7 %collective-permute-start.18 = (bf16[8,480,128]{2,1,0:T(8,128)(2,1)}, bf16[8,480,128]{2,1,0:T(8,128)(2,1)}, u32[]{:S(2)}, u32[]{:S(2)}) collective-permute-start(bf16[8,480,128]{2,1,0:T(8,128)(2,1)} %collective-permute-done.4.refs_0_), channel_id=1, source_target_pairs={{0,1},{1,0},{2,3},{3,2},{4,5},{5,4},{6,7},{7,6},{8,9},{9,8},{10,11... | collective-permute-start | bytes 2949128 | tf_op jit(solution)/shard_map/ppermute | solution.py:467
  325.1 21.0 %collective-permute-start.5 = (bf16[8,480,128]{2,1,0:T(8,128)(2,1)}, bf16[8,480,128]{2,1,0:T(8,128)(2,1)}, u32[]{:S(2)}, u32[]{:S(2)}) collective-permute-start(bf16[8,480,128]{2,1,0:T(8,128)(2,1)} %collective-permute-done.4.refs_0_), channel_id=1, source_target_pairs={{0,14},{1,3},{2,0},{3,5},{4,2},{5,7},{6,4},{7,9},{8,6},{9,11},{10,... | collective-permute-start | bytes 2949128 | tf_op jit(solution)/shard_map/ppermute | solution.py:464
  342.8 27.5 %collective-permute-start.17 = (bf16[8,480,128]{2,1,0:T(8,128)(2,1)}, bf16[8,480,128]{2,1,0:T(8,128)(2,1)}, u32[]{:S(2)}, u32[]{:S(2)}) collective-permute-start(bf16[8,480,128]{2,1,0:T(8,128)(2,1)} %collective-permute-done.13.refs_0_), channel_id=1, source_target_pairs={{0,1},{1,0},{2,3},{3,2},{4,5},{5,4},{6,7},{7,6},{8,9},{9,8},{10,11... | collective-permute-start | bytes 2949128 | tf_op jit(solution)/shard_map/ppermute | solution.py:467
  345.3 19.0 %collective-permute-start.14 = (bf16[8,480,128]{2,1,0:T(8,128)(2,1)}, bf16[8,480,128]{2,1,0:T(8,128)(2,1)}, u32[]{:S(2)}, u32[]{:S(2)}) collective-permute-start(bf16[8,480,128]{2,1,0:T(8,128)(2,1)} %collective-permute-done.13.refs_0_), channel_id=1, source_target_pairs={{0,14},{1,3},{2,0},{3,5},{4,2},{5,7},{6,4},{7,9},{8,6},{9,11},{10,... | collective-permute-start | bytes 2949128 | tf_op jit(solution)/shard_map/ppermute | solution.py:464
  346.1 32.9 %collective-permute-start.16 = (bf16[8,480,128]{2,1,0:T(8,128)(2,1)}, bf16[8,480,128]{2,1,0:T(8,128)(2,1)}, u32[]{:S(2)}, u32[]{:S(2)}) collective-permute-start(bf16[8,480,128]{2,1,0:T(8,128)(2,1)} %collective-permute-done.5.refs_0_), channel_id=1, source_target_pairs={{0,1},{1,0},{2,3},{3,2},{4,5},{5,4},{6,7},{7,6},{8,9},{9,8},{10,11... | collective-permute-start | bytes 2949128 | tf_op jit(solution)/shard_map/ppermute | solution.py:467
  346.2 24.2 %collective-permute-start.6 = (bf16[8,480,128]{2,1,0:T(8,128)(2,1)}, bf16[8,480,128]{2,1,0:T(8,128)(2,1)}, u32[]{:S(2)}, u32[]{:S(2)}) collective-permute-start(bf16[8,480,128]{2,1,0:T(8,128)(2,1)} %collective-permute-done.5.refs_0_), channel_id=1, source_target_pairs={{0,14},{1,3},{2,0},{3,5},{4,2},{5,7},{6,4},{7,9},{8,6},{9,11},{10,... | collective-permute-start | bytes 2949128 | tf_op jit(solution)/shard_map/ppermute | solution.py:464
  364.4 23.2 %collective-permute-start.15 = (bf16[8,480,128]{2,1,0:T(8,128)(2,1)}, bf16[8,480,128]{2,1,0:T(8,128)(2,1)}, u32[]{:S(2)}, u32[]{:S(2)}) collective-permute-start(bf16[8,480,128]{2,1,0:T(8,128)(2,1)} %collective-permute-done.14.refs_0_), channel_id=1, source_target_pairs={{0,1},{1,0},{2,3},{3,2},{4,5},{5,4},{6,7},{7,6},{8,9},{9,8},{10,11... | collective-permute-start | bytes 2949128 | tf_op jit(solution)/shard_map/ppermute | solution.py:467
  370.3 31.8 %collective-permute-start.7 = (bf16[8,480,128]{2,1,0:T(8,128)(2,1)}, bf16[8,480,128]{2,1,0:T(8,128)(2,1)}, u32[]{:S(2)}, u32[]{:S(2)}) collective-permute-start(bf16[8,480,128]{2,1,0:T(8,128)(2,1)} %collective-permute-done.6.refs_0_), channel_id=1, source_target_pairs={{0,1},{1,0},{2,3},{3,2},{4,5},{5,4},{6,7},{7,6},{8,9},{9,8},{10,11... | collective-permute-start | bytes 2949128 | tf_op jit(solution)/shard_map/ppermute | solution.py:467
  (1 other events, 4.0 us)
